TPU v7x, 32 devices: a whole 2x2x4 slice. The times are simulated.
32 devices in a mesh: ctx: 4 (over y, x), head: 8 (over z, core).
Axes of the slice: x: 2, y: 2, z: 4, core: 2. Of those that a mesh axis runs over, the one named last changes fastest.
Arguments:
- state: bfloat16 [4096, 2048], P('ctx'), may hold values from -6 to 6
- norm_gain: bfloat16 [2048], replicated, may hold values from 0.5 to 1.5
- w_qkv: bfloat16 [3, 2048, 2048], P(None, None, 'head'), may hold values from -2 to 2
- w_out: bfloat16 [2048, 2048], P('head'), may hold values from -0.125 to 0.125
- probe: bfloat16 [4096, 2048], P('ctx'), may hold values from -6 to 6
- noise: bfloat16 [4096, 2048], P(('ctx', 'head')), may hold values from -6 to 6
- segment_ids: int32 [4096], P('ctx'), may hold values from 0 to 2, never falling along the last dimension, each value on 1 to 3072 neighbouring positions
Outputs:
- new_state: float32 [4096, 2048], P(('ctx', 'head'))
Inputs may be any that keep to these rules, and one draw needn't show every extreme that they name: `segment_ids`: segment numbers never fall along the sequence; a segment holds at most 3072 positions.
All inputs are finite; a program needn't handle non-finite values.
Results may differ from a plain program's by a relative error of at most 0.011.
Values may be sent and summed in bfloat16 or wider, within the bound.
A program may use at most 128 MiB of HBM per device.

v0:
```python
import functools

import jax
import jax.numpy as jnp
from jax import lax
from jax.experimental import pallas as pl
from jax.experimental.pallas import tpu as pltpu
from jax.sharding import PartitionSpec as P

HEAD_DIM = 128
EPSILON = 1e-05
STEP_SIZE = 0.25
NOISE_SCALE = (2.0 * STEP_SIZE) ** 0.5
NEGATIVE = -1e30
LOG2E = 1.4426950408889634
MESH = pl.DeviceIdType.MESH
VMEM = pl.BlockSpec(memory_space=pltpu.VMEM)
ANY = pl.BlockSpec(memory_space=pl.ANY)
NT = (((1,), (1,)), ((), ()))
TN = (((0,), (0,)), ((), ()))
FORWARD_BLOCKS = (512, 512)
BACKWARD_BLOCKS = (512, 512)


def row_scale(matrix):
    return lax.rsqrt(jnp.mean(matrix * matrix, axis=-1, keepdims=True) + EPSILON)


def dot32(left, right, dims):
    return lax.dot_general(left, right, dims, preferred_element_type=jnp.float32)


def greet(axis, number, me):
    barrier = pltpu.get_barrier_semaphore()
    for step in range(1, number):
        pl.semaphore_signal(
            barrier, inc=1, device_id={axis: lax.rem(me + step, number)}, device_id_type=MESH
        )
    pl.semaphore_wait(barrier, number - 1)


def gather_kernel(
    number, key_ref, value_ref, seg_ref, normed_ref, w_ref, keys, values, segs, query_out, send_sem,
    recv_sem, own_sem,
):
    me = lax.axis_index("ctx")
    rows = key_ref.shape[0]
    greet("ctx", number, me)

    def place(index):
        return pl.ds(pl.multiple_of(index * rows, rows), rows)

    def send(slot, source, target, peer):
        copy = pltpu.make_async_remote_copy(
            src_ref=source,
            dst_ref=target,
            send_sem=send_sem.at[slot],
            recv_sem=recv_sem.at[slot],
            device_id={"ctx": peer},
            device_id_type=MESH,
        )
        copy.start()
        return copy

    mine = place(me)
    copies = []
    for step in range(1, number):
        copies.append(send(step, seg_ref, segs.at[me], lax.rem(me + step, number)))
    relay = number == 4
    if relay:
        low, high = lax.rem(me, 2), me // 2
        across, along = high * 2 + 1 - low, (1 - high) * 2 + low
        key_first = send(number, key_ref, keys.at[mine], across)
        value_first = send(number + 1, value_ref, values.at[mine], along)
        copies.append(send(number + 2, value_ref, values.at[mine], across))
        copies.append(send(number + 3, key_ref, keys.at[mine], along))
    else:
        for step in range(1, number):
            peer = lax.rem(me + step, number)
            copies.append(send(number + 2 * step, key_ref, keys.at[mine], peer))
            copies.append(send(number + 2 * step + 1, value_ref, values.at[mine], peer))
    pairs = ((key_ref, keys.at[mine]), (value_ref, values.at[mine]), (seg_ref, segs.at[me]))
    for index, (source, target) in enumerate(pairs):
        copy = pltpu.make_async_copy(source, target, own_sem.at[index])
        copy.start()
        copies.append(copy)
    tile = min(256, rows)

    def project(piece, _):
        at = pl.ds(pl.multiple_of(piece * tile, tile), tile)
        query_out[at, :] = jnp.dot(
            normed_ref[at, :], w_ref[...], preferred_element_type=jnp.float32
        ).astype(jnp.bfloat16)
        return 0

    lax.fori_loop(0, rows // tile, project, 0)
    if relay:
        key_first.wait()
        copies.append(send(number + 4, keys.at[place(across)], keys.at[place(across)], along))
        value_first.wait()
        copies.append(send(number + 5, values.at[place(along)], values.at[place(along)], across))
    for copy in copies:
        copy.wait()


def gather_keys(number, key_rows, value_rows, segment_ids, normed, w_query):
    rows, width = key_rows.shape
    seg = segment_ids.reshape(-1, 128)
    full = jax.ShapeDtypeStruct((number * rows, width), key_rows.dtype)
    keys, values, segs, queries = pl.pallas_call(
        functools.partial(gather_kernel, number),
        out_shape=(
            full,
            full,
            jax.ShapeDtypeStruct((number,) + seg.shape, seg.dtype),
            jax.ShapeDtypeStruct((rows, width), key_rows.dtype),
        ),
        in_specs=[VMEM] * 5,
        out_specs=(ANY, ANY, ANY, VMEM),
        scratch_shapes=[
            pltpu.SemaphoreType.DMA((3 * number + 6,)),
            pltpu.SemaphoreType.DMA((3 * number + 6,)),
            pltpu.SemaphoreType.DMA((3,)),
        ],
        compiler_params=pltpu.CompilerParams(collective_id=0, has_side_effects=True),
    )(key_rows, value_rows, seg, normed, w_query)
    return keys, values, segs.reshape(-1), queries


def block_ranges(table, index):
    return [table[index, column] for column in range(4)]


def forward_kernel(
    heads, bq, bk, table, query_ref, key_ref, value_ref, start_ref, pos_ref, out_ref, log_ref
):
    factor = HEAD_DIM ** (-0.5) * LOG2E
    blocks = query_ref.shape[0] // bq

    def one_block(index, _):
        low, inner_low, inner_high, high = block_ranges(table, index)
        rows = pl.ds(pl.multiple_of(index * bq, bq), bq)
        start, pos = start_ref[index], pos_ref[index]

        def step(masked, piece, carry):
            keys_at = pl.ds(pl.multiple_of(piece * bk, bk), bk)
            if masked:
                key_pos = piece * bk + lax.broadcasted_iota(jnp.int32, (bk, bq), 0)
                allowed = (key_pos >= start) & (key_pos <= pos)
            result = []
            for head in range(heads):
                top, total, acc = carry[head]
                cols = pl.ds(head * HEAD_DIM, HEAD_DIM)
                scores = dot32(key_ref[keys_at, cols], query_ref[rows, cols], NT)
                if masked:
                    scores = jnp.where(allowed, scores, NEGATIVE)
                new_top = jnp.maximum(top, jnp.max(scores, axis=0, keepdims=True) * factor)
                weights = jnp.exp2(scores * factor - new_top)
                scale = jnp.exp2(top - new_top)
                total = total * scale + jnp.sum(weights, axis=0, keepdims=True)
                acc = acc * scale + dot32(
                    value_ref[keys_at, cols], weights.astype(jnp.bfloat16), TN
                )
                result.append((new_top, total, acc))
            return tuple(result)

        carry = tuple(
            (
                jnp.full((1, bq), NEGATIVE, jnp.float32),
                jnp.zeros((1, bq), jnp.float32),
                jnp.zeros((HEAD_DIM, bq), jnp.float32),
            )
            for _ in range(heads)
        )
        carry = lax.fori_loop(low, inner_low, functools.partial(step, True), carry)
        carry = lax.fori_loop(inner_low, inner_high, functools.partial(step, False), carry)
        carry = lax.fori_loop(inner_high, high, functools.partial(step, True), carry)
        for head in range(heads):
            top, total, acc = carry[head]
            out_ref[rows, pl.ds(head * HEAD_DIM, HEAD_DIM)] = (acc / total).T.astype(jnp.bfloat16)
            log_ref[index, pl.ds(head, 1), :] = top + jnp.log2(total)
        return 0

    lax.fori_loop(0, blocks, one_block, 0)


def backward_kernel(
    heads, bq, bk, table, query_ref, key_ref, value_ref, grad_ref, out_ref, log_ref, start_ref,
    pos_ref, query_out, pair_out, pair_acc,
):
    score_scale = HEAD_DIM ** (-0.5)
    factor = score_scale * LOG2E
    blocks = query_ref.shape[0] // bq
    width = heads * HEAD_DIM
    pair_rows = pair_acc.shape[0]

    def clear(piece, _):
        at = pl.ds(pl.multiple_of(piece * bk, bk), bk)
        pair_acc[at, :] = jnp.zeros((bk, 2 * width), jnp.float32)
        return 0

    lax.fori_loop(0, pair_rows // bk, clear, 0)

    def one_block(index, _):
        low, inner_low, inner_high, high = block_ranges(table, index)
        rows = pl.ds(pl.multiple_of(index * bq, bq), bq)
        start, pos = start_ref[index], pos_ref[index]
        deltas, logs = [], []
        for head in range(heads):
            cols = pl.ds(head * HEAD_DIM, HEAD_DIM)
            product = grad_ref[rows, cols].astype(jnp.float32) * out_ref[rows, cols].astype(
                jnp.float32
            )
            deltas.append(jnp.sum(product.T, axis=0, keepdims=True))
            logs.append(log_ref[index, pl.ds(head, 1), :])

        def step(masked, piece, carry):
            keys_at = pl.ds(pl.multiple_of(piece * bk, bk), bk)
            if masked:
                key_pos = piece * bk + lax.broadcasted_iota(jnp.int32, (bk, bq), 0)
                allowed = (key_pos >= start) & (key_pos <= pos)
            result = []
            for head in range(heads):
                cols = pl.ds(head * HEAD_DIM, HEAD_DIM)
                value_cols = pl.ds(width + head * HEAD_DIM, HEAD_DIM)
                key_block, query_block = key_ref[keys_at, cols], query_ref[rows, cols]
                grad_block = grad_ref[rows, cols]
                scores = dot32(key_block, query_block, NT)
                probabilities = jnp.exp2(scores * factor - logs[head])
                if masked:
                    probabilities = jnp.where(allowed, probabilities, 0.0)
                dprobs = dot32(value_ref[keys_at, cols], grad_block, NT)
                dscores = (probabilities * (dprobs - deltas[head])).astype(jnp.bfloat16)
                pair_acc[keys_at, value_cols] += jnp.dot(
                    probabilities.astype(jnp.bfloat16),
                    grad_block,
                    preferred_element_type=jnp.float32,
                )
                pair_acc[keys_at, cols] += jnp.dot(
                    dscores, query_block, preferred_element_type=jnp.float32
                )
                result.append(carry[head] + dot32(key_block, dscores, TN))
            return tuple(result)

        carry = tuple(jnp.zeros((HEAD_DIM, bq), jnp.float32) for _ in range(heads))
        carry = lax.fori_loop(low, inner_low, functools.partial(step, True), carry)
        carry = lax.fori_loop(inner_low, inner_high, functools.partial(step, False), carry)
        carry = lax.fori_loop(inner_high, high, functools.partial(step, True), carry)
        for head in range(heads):
            query_out[rows, pl.ds(head * HEAD_DIM, HEAD_DIM)] = (
                carry[head].T * score_scale
            ).astype(jnp.bfloat16)
        return 0

    lax.fori_loop(0, blocks, one_block, 0)

    def flush(piece, _):
        at = pl.ds(pl.multiple_of(piece * bk, bk), bk)
        pair_out[at, :width] = (pair_acc[at, :width] * score_scale).astype(jnp.bfloat16)
        pair_out[at, width:] = pair_acc[at, width:].astype(jnp.bfloat16)
        return 0

    lax.fori_loop(0, pair_rows // bk, flush, 0)


def make_table(start, pos, bq, bk):
    starts, places = start.reshape(-1, bq), pos.reshape(-1, bq)
    low = starts[:, 0] // bk
    inner_low = (starts[:, -1] + bk - 1) // bk
    inner_high = jnp.maximum(inner_low, (places[:, 0] + 1) // bk)
    high = places[:, -1] // bk + 1
    return jnp.stack([low, inner_low, inner_high, high], axis=1).astype(jnp.int32)


def middle_kernel(
    number, part_ref, w_any, state_ref, probe_ref, grad_out, readout_out, w_ref, joined, half,
    sending, landing, send_sem, recv_sem, back_send, back_recv, w_sem,
):
    me = lax.axis_index("head")
    width = part_ref.shape[1]
    own = state_ref.shape[0]
    model = state_ref.shape[1]
    w_copy = pltpu.make_async_copy(w_any, w_ref, w_sem)
    w_copy.start()
    greet("head", number, me)
    my_cols = pl.ds(pl.multiple_of(me * width, width), width)
    my_rows = pl.ds(pl.multiple_of(me * own, own), own)
    copies = []
    for step in range(1, number):
        peer = lax.rem(me + step, number)
        copy = pltpu.make_async_remote_copy(
            src_ref=part_ref.at[pl.ds(pl.multiple_of(peer * own, own), own)],
            dst_ref=joined.at[:, my_cols],
            send_sem=send_sem.at[step],
            recv_sem=recv_sem.at[step],
            device_id={"head": peer},
            device_id_type=MESH,
        )
        copy.start()
        copies.append(copy)
    joined[:, my_cols] = part_ref[my_rows, :]
    w_copy.wait()
    for copy in copies:
        copy.wait()

    tile = min(256, model)

    def project(piece, carry):
        squares, products = carry
        cols = pl.ds(pl.multiple_of(piece * tile, tile), tile)
        layer = state_ref[:, cols].astype(jnp.float32) + jnp.dot(
            joined[...], w_ref[:, cols], preferred_element_type=jnp.float32
        )
        readout_out[:, cols] = layer
        squares = squares + jnp.sum(layer * layer, axis=1, keepdims=True)
        products = products + jnp.sum(
            layer * probe_ref[:, cols].astype(jnp.float32), axis=1, keepdims=True
        )
        return squares, products

    zero = jnp.zeros((own, 1), jnp.float32)
    squares, products = lax.fori_loop(0, model // tile, project, (zero, zero))
    scale = lax.rsqrt(squares / model + EPSILON)
    bend = scale**3 * (products / model)

    def finish(piece, _):
        cols = pl.ds(pl.multiple_of(piece * tile, tile), tile)
        readout = scale * probe_ref[:, cols].astype(jnp.float32) - readout_out[:, cols] * bend
        readout_out[:, cols] = readout
        half[:, cols] = readout.astype(jnp.bfloat16)
        return 0

    lax.fori_loop(0, model // tile, finish, 0)
    copies = []
    for step in range(1, number):
        peer = lax.rem(me + step, number)
        sending[step] = dot32(
            half[...], w_ref[pl.ds(pl.multiple_of(peer * width, width), width), :], NT
        ).astype(jnp.bfloat16)
        copy = pltpu.make_async_remote_copy(
            src_ref=sending.at[step],
            dst_ref=landing.at[my_rows],
            send_sem=back_send.at[step],
            recv_sem=back_recv.at[step],
            device_id={"head": peer},
            device_id_type=MESH,
        )
        copy.start()
        copies.append(copy)
    landing[my_rows, :] = dot32(half[...], w_ref[my_cols, :], NT).astype(jnp.bfloat16)
    for copy in copies:
        copy.wait()
    grad_out[...] = landing[...]


def middle(number, part, w_full, state_own, probe_own):
    rows, width = part.shape
    own, model = state_own.shape
    return pl.pallas_call(
        functools.partial(middle_kernel, number),
        out_shape=(
            jax.ShapeDtypeStruct((rows, width), jnp.bfloat16),
            jax.ShapeDtypeStruct((own, model), jnp.float32),
        ),
        in_specs=[VMEM, ANY, VMEM, VMEM],
        out_specs=(VMEM, VMEM),
        scratch_shapes=[
            pltpu.VMEM(w_full.shape, jnp.bfloat16),
            pltpu.VMEM((own, number * width), jnp.bfloat16),
            pltpu.VMEM((own, model), jnp.bfloat16),
            pltpu.VMEM((number, own, width), jnp.bfloat16),
            pltpu.VMEM((rows, width), jnp.bfloat16),
            pltpu.SemaphoreType.DMA((number,)),
            pltpu.SemaphoreType.DMA((number,)),
            pltpu.SemaphoreType.DMA((number,)),
            pltpu.SemaphoreType.DMA((number,)),
            pltpu.SemaphoreType.DMA,
        ],
        compiler_params=pltpu.CompilerParams(
            collective_id=1, has_side_effects=True, vmem_limit_bytes=60 * 2**20
        ),
    )(part, w_full, state_own, probe_own)


def tail_kernel(
    ctx_count, number, pair_any, query_ref, w_ref, sum_out, own_pair, arriving, gathered, terms,
    from_partner, reduced, landing, ctx_send, ctx_recv, p_send, p_recv, z_send, z_recv, own_sem,
):
    ctx, me = lax.axis_index("ctx"), lax.axis_index("head")
    groups = number // 2
    group, core = me // 2, lax.rem(me, 2)
    partner = group * 2 + 1 - core
    rows, width = query_ref.shape
    own, model = sum_out.shape
    chunk = 2 * own
    own_copy = pltpu.make_async_copy(
        pair_any.at[pl.ds(pl.multiple_of(ctx * rows, rows), rows)], own_pair, own_sem
    )
    own_copy.start()
    barrier = pltpu.get_barrier_semaphore()
    peers = [{"ctx": lax.rem(ctx + step, ctx_count)} for step in range(1, ctx_count)]
    peers.append({"head": partner})
    for step in range(1, groups):
        peers.append({"head": lax.rem(group + step, groups) * 2 + core})
    for peer in peers:
        pl.semaphore_signal(barrier, inc=1, device_id=peer, device_id_type=MESH)
    pl.semaphore_wait(barrier, len(peers))

    def chunk_start(order):
        dest = lax.rem(group + order + 1, groups)
        return dest, pl.multiple_of(dest * chunk, chunk)

    def ctx_copy(order, step):
        target = lax.rem(ctx - step + ctx_count, ctx_count)
        _, first = chunk_start(order)
        return pltpu.make_async_remote_copy(
            src_ref=pair_any.at[pl.ds(pl.multiple_of(target * rows + first, chunk), chunk)],
            dst_ref=arriving.at[order, step - 1],
            send_sem=ctx_send.at[order, step],
            recv_sem=ctx_recv.at[order, step],
            device_id={"ctx": target},
            device_id_type=MESH,
        )

    for order in range(groups):
        for step in range(1, ctx_count):

            @pl.when(step <= ctx)
            def _():
                ctx_copy(order, step).start()

    own_copy.wait()
    tile = min(512, model)
    mine = pl.ds(pl.multiple_of(core * own, own), own)
    theirs = pl.ds(pl.multiple_of((1 - core) * own, own), own)
    waiting = []
    for order in range(groups):
        dest, first = chunk_start(order)
        at = pl.ds(first, chunk)
        gathered[...] = own_pair[at, :].astype(jnp.float32)
        for step in range(1, ctx_count):

            @pl.when(ctx + step < ctx_count)
            def _():
                ctx_copy(order, step).wait_recv()
                gathered[...] += arriving[order, step - 1].astype(jnp.float32)

        def multiply(piece, _):
            cols = pl.ds(pl.multiple_of(piece * tile, tile), tile)
            term = dot32(query_ref[at, :], w_ref[0, cols, :], NT)
            term += dot32(gathered[:, :width].astype(jnp.bfloat16), w_ref[1, cols, :], NT)
            term += dot32(gathered[:, width:].astype(jnp.bfloat16), w_ref[2, cols, :], NT)
            terms[order, :, cols] = term.astype(jnp.bfloat16)
            return 0

        lax.fori_loop(0, model // tile, multiply, 0)
        copy = pltpu.make_async_remote_copy(
            src_ref=terms.at[order, theirs],
            dst_ref=from_partner.at[order],
            send_sem=p_send.at[order],
            recv_sem=p_recv.at[order],
            device_id={"head": partner},
            device_id_type=MESH,
        )
        copy.start()
        copy.wait()
        both = terms[order, mine, :].astype(jnp.float32) + from_partner[order].astype(jnp.float32)
        if order < groups - 1:
            reduced[order] = both.astype(jnp.bfloat16)
            copy = pltpu.make_async_remote_copy(
                src_ref=reduced.at[order],
                dst_ref=landing.at[order],
                send_sem=z_send.at[order],
                recv_sem=z_recv.at[order],
                device_id={"head": dest * 2 + core},
                device_id_type=MESH,
            )
            copy.start()
            waiting.append(copy)
        else:
            sum_out[...] = both
    for order, copy in enumerate(waiting):
        copy.wait()
        sum_out[...] += landing[order].astype(jnp.float32)
    for order in range(groups):
        for step in range(1, ctx_count):

            @pl.when(step <= ctx)
            def _():
                ctx_copy(order, step).wait_send()


def tail(ctx_count, number, pair, query_grad, w_qkv):
    rows, width = query_grad.shape
    model = w_qkv.shape[1]
    own, groups = rows // number, number // 2
    half, full = jnp.bfloat16, jnp.float32
    dma = pltpu.SemaphoreType.DMA
    return pl.pallas_call(
        functools.partial(tail_kernel, ctx_count, number),
        out_shape=jax.ShapeDtypeStruct((own, model), full),
        in_specs=[ANY, VMEM, VMEM],
        out_specs=VMEM,
        scratch_shapes=[
            pltpu.VMEM((rows, 2 * width), half),
            pltpu.VMEM((groups, ctx_count - 1, 2 * own, 2 * width), half),
            pltpu.VMEM((2 * own, 2 * width), full),
            pltpu.VMEM((groups, 2 * own, model), half),
            pltpu.VMEM((groups, own, model), half),
            pltpu.VMEM((groups, own, model), half),
            pltpu.VMEM((groups, own, model), half),
            dma((groups, ctx_count)),
            dma((groups, ctx_count)),
            dma((groups,)),
            dma((groups,)),
            dma((groups,)),
            dma((groups,)),
            dma,
        ],
        compiler_params=pltpu.CompilerParams(
            collective_id=2, has_side_effects=True, vmem_limit_bytes=60 * 2**20
        ),
    )(pair, query_grad, w_qkv)


def body(state, norm_gain, w_qkv, w_out, probe, noise, segment_ids):
    local_rows, model_width = state.shape
    width = w_qkv.shape[2]
    local_heads = width // HEAD_DIM
    head_count = lax.axis_size("head")
    ctx_count = lax.axis_size("ctx")
    ctx_index = lax.axis_index("ctx")
    own_rows = local_rows // head_count
    row_start = lax.axis_index("head") * own_rows
    w_full = lax.all_gather(w_out, "head", axis=0, tiled=True)
    state_f = state.astype(jnp.float32)
    gain_full = norm_gain.astype(jnp.float32)
    inverse = row_scale(state_f)
    normed = (state_f * inverse * gain_full).astype(jnp.bfloat16)

    def project(index):
        return jnp.dot(normed, w_qkv[index], preferred_element_type=jnp.float32).astype(
            jnp.bfloat16
        )

    key_rows, value_rows = project(1), project(2)
    keys, values, segs, query_rows = gather_keys(
        ctx_count, key_rows, value_rows, segment_ids, normed, w_qkv[0]
    )
    total_rows = keys.shape[0]
    pos = ctx_index * local_rows + jnp.arange(local_rows, dtype=jnp.int32)
    start = jnp.sum((segs[None, :] < segment_ids[:, None]).astype(jnp.int32), axis=1)
    fq, fk = (min(local_rows, size) for size in FORWARD_BLOCKS)
    gq, gk = (min(local_rows, size) for size in BACKWARD_BLOCKS)
    smem = pl.BlockSpec(memory_space=pltpu.SMEM)
    params = pltpu.CompilerParams(vmem_limit_bytes=60 * 2**20)
    outputs, logs = pl.pallas_call(
        functools.partial(forward_kernel, local_heads, fq, fk),
        out_shape=(
            jax.ShapeDtypeStruct((local_rows, width), jnp.bfloat16),
            jax.ShapeDtypeStruct((local_rows // fq, local_heads, fq), jnp.float32),
        ),
        in_specs=[smem] + [VMEM] * 5,
        out_specs=(VMEM, VMEM),
        compiler_params=params,
        cost_estimate=pl.CostEstimate(
            flops=4 * local_rows * total_rows * width, bytes_accessed=0, transcendentals=0
        ),
    )(
        make_table(start, pos, fq, fk),
        query_rows,
        keys,
        values,
        start.reshape(-1, 1, fq),
        pos.reshape(-1, 1, fq),
    )
    state_half = lax.dynamic_slice_in_dim(state, row_start, own_rows, 0)
    probe_own = lax.dynamic_slice_in_dim(probe, row_start, own_rows, 0)
    state_own = state_half.astype(jnp.float32)
    inverse_own = row_scale(state_own)
    grads_out, readout_own = middle(head_count, outputs, w_full, state_half, probe_own)
    query_grad, pair = pl.pallas_call(
        functools.partial(backward_kernel, local_heads, gq, gk),
        out_shape=(
            jax.ShapeDtypeStruct((local_rows, width), jnp.bfloat16),
            jax.ShapeDtypeStruct((total_rows, 2 * width), jnp.bfloat16),
        ),
        in_specs=[smem] + [VMEM] * 8,
        out_specs=(VMEM, VMEM),
        scratch_shapes=[pltpu.VMEM((total_rows, 2 * width), jnp.float32)],
        compiler_params=params,
        cost_estimate=pl.CostEstimate(
            flops=10 * local_rows * total_rows * width, bytes_accessed=0, transcendentals=0
        ),
    )(
        make_table(start, pos, gq, gk),
        query_rows,
        keys,
        values,
        grads_out,
        outputs,
        logs.reshape(local_rows // fq, local_heads, fq),
        start.reshape(-1, 1, gq),
        pos.reshape(-1, 1, gq),
    )
    normed_grad = tail(ctx_count, head_count, pair, query_grad, w_qkv)
    gain_grad = normed_grad * gain_full
    gradient = (
        readout_own
        + inverse_own * gain_grad
        - state_own * inverse_own**3 * jnp.mean(gain_grad * state_own, axis=-1, keepdims=True)
    )
    return state_own - STEP_SIZE * gradient + jnp.sqrt(2.0 * STEP_SIZE) * noise.astype(jnp.float32)


def remote(source, target, send_sem, recv_sem, ctx, head):
    return pltpu.make_async_remote_copy(
        src_ref=source,
        dst_ref=target,
        send_sem=send_sem,
        recv_sem=recv_sem,
        device_id={"ctx": ctx, "head": head},
        device_id_type=MESH,
    )


def place():
    ctx, me = lax.axis_index("ctx"), lax.axis_index("head")
    return ctx, me, me // 2, lax.rem(me, 2)


def announce(peers):
    barrier = pltpu.get_barrier_semaphore()
    for ctx, head in peers:
        pl.semaphore_signal(
            barrier, inc=1, device_id={"ctx": ctx, "head": head}, device_id_type=MESH
        )


def await_all(peers):
    pl.semaphore_wait(pltpu.get_barrier_semaphore(), len(peers))


def meet(peers):
    announce(peers)
    await_all(peers)


def far_first(groups, group, step):
    result = 0
    for index in range(groups):
        order = sorted(range(groups), key=lambda other: (-abs(other - index), -other))
        result = jnp.where(group == index, order[step], result)
    return result


def front_kernel(
    ctx_count, head_count, state_any, w_any, gain_ref, seg_ref, w_out_any, probe_any, query_any,
    kv_any, segs_out, part_any, log_out, grad_out, readout_any, w_pair, state_v, w_v, query_buf,
    kv_buf, w_ref, joined, half, sending, state_own, probe_own, query_out, kv_out, part_out,
    readout_out, load_sem, w_sem, q_send, q_recv, kv_send, kv_recv, pass_send, seg_send, seg_recv,
    line_send, line_recv, plane_send, plane_recv, beside_send, beside_recv, shard_send, shard_recv,
    shard_sem, out_send, out_recv, back_send, back_recv, own_sem, row_sem, pair_send, pair_recv,
    leave_sem,
):
    ctx, me, group, core = place()
    rows, model = state_any.shape
    own, groups = rows // head_count, head_count // 2
    slots = w_any.shape[2] // HEAD_DIM
    chunk = 2 * own
    partner = group * 2 + 1 - core

    def at(piece):
        return pl.ds(pl.multiple_of(piece * chunk, chunk), chunk)

    def own_at(piece):
        return pl.ds(pl.multiple_of(piece * own, own), own)

    def load_state(piece):
        return pltpu.make_async_copy(
            state_any.at[at(piece)], state_v.at[at(piece)], load_sem.at[piece]
        )

    load_state(0).start()
    w_loads = [pltpu.make_async_copy(w_any.at[t], w_v.at[t], w_sem.at[t]) for t in range(3)]
    for copy in w_loads:
        copy.start()
    for piece in range(1, groups):
        load_state(piece).start()
    my_rows = own_at(me)
    shard = w_out_any.shape[0]
    part, quarter = shard // 2, shard // ctx_count
    later_loads = [
        pltpu.make_async_copy(state_any.at[my_rows], state_own, row_sem.at[0]),
        pltpu.make_async_copy(probe_any.at[my_rows], probe_own, row_sem.at[1]),
        pltpu.make_async_copy(
            w_out_any, w_ref.at[pl.ds(pl.multiple_of(me * shard, shard), shard)], shard_sem
        ),
    ]
    for copy in later_loads:
        copy.start()
    peers = [(lax.rem(ctx + step, ctx_count), partner) for step in range(ctx_count)]
    for far in range(groups):
        for step in range(ctx_count):
            if far or step:
                peers.append(
                    (lax.rem(ctx + step, ctx_count), lax.rem(group + far, groups) * 2 + core)
                )
    announce(peers)

    low, high = lax.rem(ctx, 2), ctx // 2
    which = lax.rem(low + high, 2)
    across, along = high * 2 + 1 - low, (1 - high) * 2 + low

    def shard_rows(origin, first, size):
        return pl.ds(pl.multiple_of((origin * 2 + core) * shard + first, size), size)

    def line_copy(way, origin, axis, mine):
        first = which * part + axis * quarter
        here = shard_rows(origin, first, quarter)
        source = (
            w_out_any.at[pl.ds(pl.multiple_of(first, quarter), quarter)] if mine else w_ref.at[here]
        )
        other = group + 1 if way == 0 else group - 1
        return remote(
            source, w_ref.at[here], line_send.at[way, axis, origin], line_recv.at[axis, origin],
            ctx, other * 2 + core,
        )

    def plane_copy(axis, origin, kept):
        here = shard_rows(origin, kept * part + axis * quarter, quarter)
        return remote(
            w_ref.at[here], w_ref.at[here], plane_send.at[axis, origin],
            plane_recv.at[axis, origin], along if axis else across, me,
        )

    def beside_copy(kind, origin):
        kept = which if kind < 2 else 1 - which
        here = shard_rows(origin, kept * part + (kind % 2) * quarter, quarter)
        return remote(
            w_ref.at[here], w_ref.at[here], beside_send.at[kind, origin],
            beside_recv.at[kind, origin], ctx, partner,
        )

    def shard_copy():
        return remote(
            w_out_any, w_ref.at[pl.ds(pl.multiple_of(me * shard, shard), shard)], shard_send,
            shard_recv, ctx, partner,
        )

    has_up, has_down = group < groups - 1, group > 0

    def each_origin(distance, work):
        for way in range(2):
            origin = group - distance if way == 0 else group + distance

            @pl.when(origin >= 0 if way == 0 else origin < groups)
            def _():
                work(way, origin)

    def line_arrived(distance, axis):
        def work(way, origin):
            line_copy(way, origin, axis, False).wait_recv()

            @pl.when(has_up if way == 0 else has_down)
            def _():
                line_copy(way, origin, axis, False).start()

            plane_copy(axis, origin, which).start()
            beside_copy(axis, origin).start()

        each_origin(distance, work)

    def plane_arrived(distance, axis):
        def work(way, origin):
            plane_copy(axis, origin, 1 - which).wait_recv()
            beside_copy(2 + axis, origin).start()

        each_origin(distance, work)

    def weights_sent(distance):
        def work(way, origin):
            for axis in range(2):

                @pl.when(has_up if way == 0 else has_down)
                def _():
                    line_copy(way, origin, axis, False).wait_send()

                plane_copy(axis, origin, which).wait_send()
            for kind in range(4):
                beside_copy(kind, origin).wait_send()

        each_origin(distance, work)

    def own_lines(work):
        for axis in range(2):

            @pl.when(has_up)
            def _():
                work(line_copy(0, group, axis, True))

            @pl.when(has_down)
            def _():
                work(line_copy(1, group, axis, True))

    for copy in w_loads:
        copy.wait()
    gain = gain_ref[...].astype(jnp.float32).reshape(1, model)

    def away(slot, kind, piece, dest):
        head = group * 2 + kind
        return (
            remote(
                query_buf.at[slot, piece, kind], query_out.at[ctx, own_at(piece)],
                q_send.at[slot, kind, piece], q_recv.at[ctx, piece], dest, head,
            ),
            remote(
                kv_buf.at[slot, kind, piece], kv_out.at[kind, ctx, at(piece)],
                kv_send.at[slot, kind, piece], kv_recv.at[kind, ctx, piece], dest, head,
            ),
        )

    def beside(slot, piece):
        result = [
            remote(
                query_buf.at[slot, piece, 1 - core], query_out.at[ctx, own_at(piece)],
                q_send.at[slot, 1 - core, piece], q_recv.at[ctx, piece], ctx, partner,
            )
        ]
        for kind in range(2):
            result.append(
                remote(
                    kv_buf.at[slot, kind, piece], kv_out.at[kind, ctx, at(piece)],
                    kv_send.at[slot, kind, piece], kv_recv.at[kind, ctx, piece], ctx, partner,
                )
            )
        return result

    def project(piece):
        load_state(piece).wait()
        block = state_v[at(piece), :].astype(jnp.float32)
        normed = (block * row_scale(block) * gain).astype(jnp.bfloat16)
        for t in range(3):
            result = jnp.dot(normed, w_v[t], preferred_element_type=jnp.float32).astype(
                jnp.bfloat16
            )
            for slot in range(slots):
                cut = result[:, slot * HEAD_DIM : (slot + 1) * HEAD_DIM]
                if t == 0:
                    query_buf[slot, piece, 0] = cut[:own]
                    query_buf[slot, piece, 1] = cut[own:]
                else:
                    kv_buf[slot, t - 1, piece] = cut

    def send_heads(piece):
        for slot in range(slots):
            dest = core * slots + slot

            @pl.when(dest != ctx)
            def _():
                for kind in range(2):
                    for copy in away(slot, kind, piece, dest):
                        copy.start()

            @pl.when(dest == ctx)
            def _():
                query_out[ctx, own_at(piece), :] = query_buf[slot, piece, core]
                for kind in range(2):
                    kv_out[kind, ctx, at(piece), :] = kv_buf[slot, kind, piece]
                for copy in beside(slot, piece):
                    copy.start()

    project(0)
    await_all(peers)
    own_lines(lambda copy: copy.start())
    send_heads(0)
    shard_copy().start()
    segs = []
    for step in range(1, ctx_count):
        copy = remote(
            seg_ref, segs_out.at[ctx], seg_send.at[step], seg_recv.at[step],
            lax.rem(ctx + step, ctx_count), me,
        )
        copy.start()
        segs.append(copy)
    segs_out[ctx] = seg_ref[...]

    def project_and_send(piece, _):
        project(piece)
        send_heads(piece)
        return 0

    lax.fori_loop(1, groups, project_and_send, 0)

    def hand_over(piece, step):
        source = lax.rem(ctx + step, ctx_count)
        return remote(
            kv_out.at[core, source, at(piece)], kv_out.at[core, source, at(piece)],
            pass_send.at[step, piece], kv_recv.at[core, source, piece], ctx, partner,
        )

    for piece in range(groups):
        for step in range(1, ctx_count):
            copy = hand_over(piece, step)
            copy.wait_recv()
            copy.start()
        if piece == 0:
            line_arrived(1, 0)
        if piece == min(2, groups - 1):
            line_arrived(1, 1)
    line_arrived(2, 0)

    def got_query(source, piece):
        remote(
            query_out.at[source, own_at(piece)], query_out.at[source, own_at(piece)],
            q_send.at[0, 0, piece], q_recv.at[source, piece], ctx, partner,
        ).wait_recv()

    def got_kv(kind, source, piece):
        remote(
            kv_out.at[kind, source, at(piece)], kv_out.at[kind, source, at(piece)],
            kv_send.at[0, 0, piece], kv_recv.at[kind, source, piece], ctx, partner,
        ).wait_recv()

    def gather(piece, _):
        for step in range(1, ctx_count):
            source = lax.rem(ctx + step, ctx_count)
            got_query(source, piece)
            got_kv(1 - core, source, piece)
            hand_over(piece, step).wait_send()

        @pl.when(ctx // slots != core)
        def _():
            got_query(ctx, piece)
            for kind in range(2):
                got_kv(kind, ctx, piece)

        return 0

    lax.fori_loop(0, groups, gather, 0)
    for copy in segs:
        copy.wait()
    leaving = [
        pltpu.make_async_copy(query_out, query_any, leave_sem.at[0]),
        pltpu.make_async_copy(kv_out, kv_any, leave_sem.at[1]),
    ]
    for copy in leaving:
        copy.start()
    pair_copy = remote(w_any, w_pair, pair_send, pair_recv, ctx, partner)
    pair_copy.start()

    def cols_of(group_at, ctx_at):
        head = group_at * ctx_count + ctx_at
        return pl.ds(pl.multiple_of(head * HEAD_DIM, HEAD_DIM), HEAD_DIM)

    factor = HEAD_DIM ** (-0.5) * LOG2E
    sub = groups * own
    seg_all = segs_out[...]

    def below(value):
        count = jnp.where(seg_all < value, 1.0, 0.0)
        for axis in (0, 1, 2):
            count = jnp.sum(count, axis=axis, keepdims=True)
        return count[0]

    first_bound, second_bound = below(1), below(2)
    lane = lax.broadcasted_iota(jnp.int32, (1, sub), 1)
    inside = (lane // own) * (2 * own) + core * own + lane % own
    key_row = lax.broadcasted_iota(jnp.int32, (rows, sub), 0)

    def out_copy(tile, order, other):
        return remote(
            part_out.at[tile, own_at(other)], joined.at[:, cols_of(group, ctx)],
            out_send.at[tile, order], out_recv.at[group, ctx], tile, other * 2 + core,
        )

    def one_tile(tile, _):
        query = query_out[tile]
        pos = (tile * rows + inside).astype(jnp.float32)
        start = jnp.where(
            pos >= second_bound, second_bound, jnp.where(pos >= first_bound, first_bound, 0.0)
        ).astype(jnp.int32)

        def step(diagonal, piece, carry):
            top, total, acc = carry
            scores = dot32(kv_out[0, piece], query, NT)
            allowed = key_row >= start - piece * rows
            if diagonal:
                allowed = allowed & (key_row <= inside)
            scores = jnp.where(allowed, scores, NEGATIVE)
            new_top = jnp.maximum(top, jnp.max(scores, axis=0, keepdims=True) * factor)
            weights = jnp.exp2(scores * factor - new_top)
            scale = jnp.exp2(top - new_top)
            total = total * scale + jnp.sum(weights, axis=0, keepdims=True)
            acc = acc * scale + dot32(kv_out[1, piece], weights.astype(jnp.bfloat16), TN)
            return new_top, total, acc

        carry = (
            jnp.full((1, sub), NEGATIVE, jnp.float32),
            jnp.zeros((1, sub), jnp.float32),
            jnp.zeros((HEAD_DIM, sub), jnp.float32),
        )
        carry = lax.fori_loop(0, tile, functools.partial(step, False), carry)
        top, total, acc = step(True, tile, carry)
        part_out[tile] = (acc / total).T.astype(jnp.bfloat16)
        log_out[tile] = top + jnp.log2(total)
        for order in range(groups):
            other = far_first(groups, group, order)
            if order == groups - 1:

                @pl.when(tile != ctx)
                def _():
                    out_copy(tile, order, other).start()

                @pl.when(tile == ctx)
                def _():
                    joined[:, cols_of(group, ctx)] = part_out[tile, own_at(group), :]

            else:
                out_copy(tile, order, other).start()

        @pl.when(tile == 1)
        def _():
            line_arrived(2, 1)

        return 0

    lax.fori_loop(0, ctx_count, one_tile, 0)
    leaving.append(pltpu.make_async_copy(part_out, part_any, leave_sem.at[2]))
    leaving[-1].start()
    for copy in later_loads:
        copy.wait()
    sources = []
    for far in range(groups):
        for step in range(ctx_count):
            if far or step:
                sources.append((lax.rem(group + far, groups), lax.rem(ctx + step, ctx_count)))
    tile = min(256, model)
    wide = ctx_count * HEAD_DIM
    zero = jnp.zeros((own, 1), jnp.float32)
    for axis in range(2):
        plane_arrived(1, axis)
    for distance in range(3, groups):
        line_arrived(distance, 0)
    for axis in range(2):
        plane_arrived(2, axis)
    for distance in range(3, groups):
        line_arrived(distance, 1)
    shard_copy().wait_recv()

    def heads_arrived(order):
        other = far_first(groups, group, order)
        if order < groups - 1:
            for kind in range(4):
                beside_copy(kind, other).wait_recv()
        for step in range(ctx_count):
            if order < groups - 1 or step:
                peer = lax.rem(ctx + step, ctx_count)
                remote(
                    part_out.at[0, own_at(0)], joined.at[:, cols_of(other, peer)],
                    out_send.at[0, 0], out_recv.at[other, peer], peer, other * 2 + core,
                ).wait_recv()

    for order in range(groups - 1, 0, -1):
        heads_arrived(order)
    farthest = far_first(groups, group, 0)
    near = pl.ds(pl.multiple_of(jnp.where(farthest == 0, wide, 0), wide), model - wide)
    far = pl.ds(pl.multiple_of(farthest * wide, wide), wide)

    def near_layer(piece, _):
        cols = pl.ds(pl.multiple_of(piece * tile, tile), tile)
        readout_out[:, cols] = state_own[:, cols].astype(jnp.float32) + jnp.dot(
            joined[:, near], w_ref[near, cols], preferred_element_type=jnp.float32
        )
        return 0

    lax.fori_loop(0, model // tile, near_layer, 0)
    for distance in range(3, groups):
        for axis in range(2):
            plane_arrived(distance, axis)
    heads_arrived(0)

    def layer(piece, carry):
        squares, products = carry
        cols = pl.ds(pl.multiple_of(piece * tile, tile), tile)
        result = readout_out[:, cols] + jnp.dot(
            joined[:, far], w_ref[far, cols], preferred_element_type=jnp.float32
        )
        readout_out[:, cols] = result
        squares = squares + jnp.sum(result * result, axis=1, keepdims=True)
        products = products + jnp.sum(
            result * probe_own[:, cols].astype(jnp.float32), axis=1, keepdims=True
        )
        return squares, products

    squares, products = lax.fori_loop(0, model // tile, layer, (zero, zero))
    scale = lax.rsqrt(squares / model + EPSILON)
    bend = scale**3 * (products / model)

    def finish(piece, _):
        cols = pl.ds(pl.multiple_of(piece * tile, tile), tile)
        readout = scale * probe_own[:, cols].astype(jnp.float32) - readout_out[:, cols] * bend
        readout_out[:, cols] = readout
        half[:, cols] = readout.astype(jnp.bfloat16)
        return 0

    lax.fori_loop(0, model // tile, finish, 0)
    leaving.append(pltpu.make_async_copy(readout_out, readout_any, leave_sem.at[3]))
    leaving[-1].start()
    copies = []
    for order in range(groups):
        other = far_first(groups, group, order)
        result = dot32(
            half[...], w_ref[pl.ds(pl.multiple_of(other * wide, wide), wide), :], NT
        ).astype(jnp.bfloat16)
        for index in range(ctx_count):
            sending[order, index] = result[:, index * HEAD_DIM : (index + 1) * HEAD_DIM]
        for step in range(ctx_count):
            peer = lax.rem(ctx + step, ctx_count)
            if order == groups - 1 and step == 0:
                continue
            copy = remote(
                sending.at[order, peer], grad_out.at[ctx, group], back_send.at[order, step],
                back_recv.at[ctx, group], peer, other * 2 + core,
            )
            copy.start()
            copies.append(copy)
    last = pltpu.make_async_copy(sending.at[groups - 1, ctx], grad_out.at[ctx, group], own_sem)
    last.start()

    def sent(piece, _):
        for slot in range(slots):
            dest = core * slots + slot

            @pl.when(dest != ctx)
            def _():
                for kind in range(2):
                    for copy in away(slot, kind, piece, dest):
                        copy.wait_send()

            @pl.when(dest == ctx)
            def _():
                for copy in beside(slot, piece):
                    copy.wait_send()

        return 0

    lax.fori_loop(0, groups, sent, 0)

    own_lines(lambda copy: copy.wait_send())
    shard_copy().wait_send()
    for distance in range(1, groups):
        weights_sent(distance)

    def parts_sent(tile, _):
        for order in range(groups):
            other = far_first(groups, group, order)
            if order == groups - 1:

                @pl.when(tile != ctx)
                def _():
                    out_copy(tile, order, other).wait_send()

            else:
                out_copy(tile, order, other).wait_send()
        return 0

    lax.fori_loop(0, ctx_count, parts_sent, 0)
    for other, peer in sources:
        remote(
            sending.at[0, 0], grad_out.at[peer, other], back_send.at[0, 0],
            back_recv.at[peer, other], peer, other * 2 + core,
        ).wait_recv()
    for copy in copies:
        copy.wait_send()
    last.wait()
    for copy in leaving:
        copy.wait()
    pair_copy.wait()


def front(ctx_count, head_count, state, w_qkv, gain, segment_ids, w_out, probe):
    rows, model = state.shape
    width = w_qkv.shape[2]
    own, groups, slots = rows // head_count, head_count // 2, width // HEAD_DIM
    seg = segment_ids.reshape(-1, 128)
    half, full, dma = jnp.bfloat16, jnp.float32, pltpu.SemaphoreType.DMA
    shape = jax.ShapeDtypeStruct
    return pl.pallas_call(
        functools.partial(front_kernel, ctx_count, head_count),
        out_shape=(
            shape((ctx_count, groups * own, HEAD_DIM), half),
            shape((2, ctx_count, rows, HEAD_DIM), half),
            shape((ctx_count,) + seg.shape, seg.dtype),
            shape((ctx_count, groups * own, HEAD_DIM), half),
            shape((ctx_count, 1, groups * own), full),
            shape((ctx_count, groups, own, HEAD_DIM), half),
            shape((own, model), full),
            shape(w_qkv.shape, half),
        ),
        in_specs=[ANY, ANY, VMEM, VMEM, ANY, ANY],
        out_specs=(ANY, ANY, VMEM, ANY, VMEM, ANY, ANY, ANY),
        scratch_shapes=[
            pltpu.VMEM((rows, model), half),
            pltpu.VMEM(w_qkv.shape, half),
            pltpu.VMEM((slots, groups, 2, own, HEAD_DIM), half),
            pltpu.VMEM((slots, 2, groups, 2 * own, HEAD_DIM), half),
            pltpu.VMEM((model, model), half),
            pltpu.VMEM((own, model), half),
            pltpu.VMEM((own, model), half),
            pltpu.VMEM((groups, ctx_count, own, HEAD_DIM), half),
            pltpu.VMEM((own, model), half),
            pltpu.VMEM((own, model), half),
            pltpu.VMEM((ctx_count, groups * own, HEAD_DIM), half),
            pltpu.VMEM((2, ctx_count, rows, HEAD_DIM), half),
            pltpu.VMEM((ctx_count, groups * own, HEAD_DIM), half),
            pltpu.VMEM((own, model), full),
            dma((groups,)),
            dma((3,)),
            dma((slots, 2, groups)),
            dma((ctx_count, groups)),
            dma((slots, 2, groups)),
            dma((2, ctx_count, groups)),
            dma((ctx_count, groups)),
            dma((ctx_count,)),
            dma((ctx_count,)),
            dma((2, 2, groups)),
            dma((2, groups)),
            dma((2, groups)),
            dma((2, groups)),
            dma((4, groups)),
            dma((4, groups)),
            dma,
            dma,
            dma,
            dma((ctx_count, groups)),
            dma((groups, ctx_count)),
            dma((groups, ctx_count)),
            dma((ctx_count, groups)),
            dma,
            dma((2,)),
            dma,
            dma,
            dma((4,)),
        ],
        compiler_params=pltpu.CompilerParams(
            collective_id=0, has_side_effects=True, vmem_limit_bytes=62 * 2**20
        ),
    )(state, w_qkv, gain, seg, w_out, probe)


def segment_bounds(segs_ref):
    segs = segs_ref[...]

    def below(value):
        return jnp.sum(jnp.where(segs < value, 1.0, 0.0)).astype(jnp.int32)

    return below(1), below(2)


def tile_plan(bounds, rows, own, parts, sub, bk, tile, core):
    first_bound, second_bound = bounds

    def start_of(pos):
        return jnp.where(pos >= second_bound, second_bound, jnp.where(pos >= first_bound, first_bound, 0))

    blocks = sub // own
    base = tile * rows + core * own
    places = []
    for part in range(parts):
        lane = lax.broadcasted_iota(jnp.int32, (1, sub), 1)
        pos = base + (lane // own + part * blocks) * (2 * own) + lane % own
        places.append((start_of(pos), pos))
    first, last = base, base + (parts * blocks - 1) * 2 * own + own - 1
    low = start_of(first) // bk
    inner_low = (start_of(last) + bk - 1) // bk
    inner_high = jnp.maximum(inner_low, (first + 1) // bk)
    high = last // bk + 1
    return places, low, inner_low, inner_high, high


def head_backward_kernel(
    rows, own, parts, sub, bk, segs_ref, query_ref, kv_ref, grad_ref, out_ref, log_ref, query_out,
    pair_out, pair_acc,
):
    score_scale = HEAD_DIM ** (-0.5)
    factor = score_scale * LOG2E
    core = lax.rem(lax.axis_index("head"), 2)
    bounds = segment_bounds(segs_ref)
    tiles = query_ref.shape[0] // (parts * sub)
    pair_rows = pair_acc.shape[0]

    def clear(piece, _):
        at = pl.ds(pl.multiple_of(piece * bk, bk), bk)
        pair_acc[at, :] = jnp.zeros((bk, 2 * HEAD_DIM), jnp.float32)
        return 0

    lax.fori_loop(0, pair_rows // bk, clear, 0)

    def one_tile(tile, _):
        places, low, inner_low, inner_high, high = tile_plan(
            bounds, rows, own, parts, sub, bk, tile, core
        )

        def at(part):
            return pl.ds(pl.multiple_of((tile * parts + part) * sub, sub), sub)

        deltas, logs = [], []
        for part in range(parts):
            product = grad_ref[at(part), :].astype(jnp.float32) * out_ref[at(part), :].astype(
                jnp.float32
            )
            deltas.append(jnp.sum(product.T, axis=0, keepdims=True))
            logs.append(log_ref[tile, pl.ds(part, 1), :])

        def step(masked, piece, carry):
            keys_at = pl.ds(pl.multiple_of(piece * bk, bk), bk)
            if masked:
                key_pos = piece * bk + lax.broadcasted_iota(jnp.int32, (bk, sub), 0)
            result = []
            key_block, value_block = kv_ref[0, keys_at, :], kv_ref[1, keys_at, :]
            for part in range(parts):
                query_block, grad_block = query_ref[at(part), :], grad_ref[at(part), :]
                scores = dot32(key_block, query_block, NT)
                probabilities = jnp.exp2(scores * factor - logs[part])
                if masked:
                    start, pos = places[part]
                    probabilities = jnp.where(
                        (key_pos >= start) & (key_pos <= pos), probabilities, 0.0
                    )
                dprobs = dot32(value_block, grad_block, NT)
                dscores = (probabilities * (dprobs - deltas[part])).astype(jnp.bfloat16)
                pair_acc[keys_at, HEAD_DIM:] += jnp.dot(
                    probabilities.astype(jnp.bfloat16),
                    grad_block,
                    preferred_element_type=jnp.float32,
                )
                pair_acc[keys_at, :HEAD_DIM] += jnp.dot(
                    dscores, query_block, preferred_element_type=jnp.float32
                )
                result.append(carry[part] + dot32(key_block, dscores, TN))
            return tuple(result)

        carry = tuple(jnp.zeros((HEAD_DIM, sub), jnp.float32) for _ in range(parts))
        carry = lax.fori_loop(low, inner_low, functools.partial(step, True), carry)
        carry = lax.fori_loop(inner_low, inner_high, functools.partial(step, False), carry)
        carry = lax.fori_loop(inner_high, high, functools.partial(step, True), carry)
        for part in range(parts):
            query_out[at(part), :] = (carry[part].T * score_scale).astype(jnp.bfloat16)
        return 0

    lax.fori_loop(0, tiles, one_tile, 0)

    def flush(piece, _):
        at = pl.ds(pl.multiple_of(piece * bk, bk), bk)
        pair_out[at, :HEAD_DIM] = (pair_acc[at, :HEAD_DIM] * score_scale).astype(jnp.bfloat16)
        pair_out[at, HEAD_DIM:] = pair_acc[at, HEAD_DIM:].astype(jnp.bfloat16)
        return 0

    lax.fori_loop(0, pair_rows // bk, flush, 0)


def finish_kernel(
    ctx_count, head_count, query_ref, pair_ref, w_any, w_pair, state_any, noise_ref, readout_ref,
    gain_ref, new_out, w_both, beside, away, terms_in, partial, sending, total, state_own, b_send,
    b_recv, a_send, a_recv, z_send, z_recv, own_sem,
):
    ctx, me, group, core = place()
    groups = head_count // 2
    own, model = new_out.shape
    slots = ctx_count // 2
    partner = group * 2 + 1 - core
    my_rows = pl.ds(pl.multiple_of(me * own, own), own)
    loads = [
        pltpu.make_async_copy(w_any, w_both.at[core], own_sem.at[0]),
        pltpu.make_async_copy(w_pair, w_both.at[1 - core], own_sem.at[1]),
        pltpu.make_async_copy(state_any.at[my_rows], state_own, own_sem.at[2]),
    ]
    for copy in loads:
        copy.start()
    peers = [(ctx, partner)]
    peers += [(lax.rem(ctx + step, ctx_count), me) for step in range(1, ctx_count)]
    peers += [(ctx, lax.rem(group + far, groups) * 2 + core) for far in range(1, groups)]
    meet(peers)
    dests = [far_first(groups, group, order) for order in range(groups)]
    copies = []
    for order, dest in enumerate(dests):
        copy = remote(
            pair_ref.at[:, dest, 1 - core], beside.at[order], b_send.at[order], b_recv.at[order],
            ctx, partner,
        )
        copy.start()
        copies.append(copy)

    def stripe(source):
        slot = lax.rem(source, slots)
        return pl.ds(pl.multiple_of(slot * HEAD_DIM, HEAD_DIM), HEAD_DIM)

    def exchange(order, dest, step):
        peer = lax.rem(ctx + step, ctx_count)
        return remote(
            away.at[order, step], terms_in.at[dest, ctx // slots, :, :, stripe(ctx)],
            a_send.at[order, step], a_recv.at[dest, ctx], peer, me,
        )

    def arrived(dest, step):
        source = lax.rem(ctx + step, ctx_count)
        remote(
            away.at[0, 0], terms_in.at[dest, source // slots, :, :, stripe(source)],
            a_send.at[0, 0], a_recv.at[dest, source], source, me,
        ).wait_recv()

    for order, dest in enumerate(dests):
        copies[order].wait_recv()
        for step in range(1, ctx_count):
            peer = lax.rem(ctx + step, ctx_count)
            pair = pair_ref[peer, dest, core].astype(jnp.float32) + beside[order, peer].astype(
                jnp.float32
            )
            pair = pair.astype(jnp.bfloat16)
            away[order, step, 0] = query_ref[peer, dest]
            away[order, step, 1] = pair[:, :HEAD_DIM]
            away[order, step, 2] = pair[:, HEAD_DIM:]
            exchange(order, dest, step).start()
        pair = pair_ref[ctx, dest, core].astype(jnp.float32) + beside[order, ctx].astype(
            jnp.float32
        )
        pair = pair.astype(jnp.bfloat16)
        at = stripe(ctx)
        terms_in[dest, ctx // slots, 0, :, at] = query_ref[ctx, dest]
        terms_in[dest, ctx // slots, 1, :, at] = pair[:, :HEAD_DIM]
        terms_in[dest, ctx // slots, 2, :, at] = pair[:, HEAD_DIM:]
    for copy in loads:
        copy.wait()
    pieces = partial.shape[2]
    tile = model // pieces

    def chain(order, dest, piece):
        up = dest > group
        line = jnp.where(up, 0, 1)
        peer = jnp.where(up, group + 1, group - 1)
        return remote(
            sending.at[order, piece], partial.at[line, dest, piece], z_send.at[order, piece],
            z_recv.at[line, dest, piece], ctx, peer * 2 + core,
        )

    def came(line, dest, piece):
        remote(
            sending.at[0, piece], partial.at[line, dest, piece], z_send.at[0, piece],
            z_recv.at[line, dest, piece], ctx, partner,
        ).wait_recv()

    def term(dest, piece):
        cols = pl.ds(pl.multiple_of(piece * tile, tile), tile)
        result = None
        for half in range(2):
            for kind in range(3):
                part = dot32(terms_in[dest, half, kind], w_both[half, kind, cols, :], NT)
                result = part if result is None else result + part
        return result

    for order, dest in enumerate(dests[:-1]):
        for step in range(1, ctx_count):
            arrived(dest, step)
        line = jnp.where(dest > group, 0, 1)
        inner = (group > 0) & (group < groups - 1)

        def one_piece(piece, _):
            total[...] = term(dest, piece)

            @pl.when(inner)
            def _():
                came(line, dest, piece)
                total[...] += partial[line, dest, piece].astype(jnp.float32)

            sending[order, piece] = total[...].astype(jnp.bfloat16)
            chain(order, dest, piece).start()
            return 0

        lax.fori_loop(0, pieces, one_piece, 0)

    for step in range(1, ctx_count):
        arrived(group, step)

    state = state_own[...].astype(jnp.float32)
    inverse = row_scale(state)

    def last_piece(piece, slope):
        cols = pl.ds(pl.multiple_of(piece * tile, tile), tile)
        total[...] = term(group, piece)

        @pl.when(group > 0)
        def _():
            came(0, group, piece)
            total[...] += partial[0, group, piece].astype(jnp.float32)

        @pl.when(group < groups - 1)
        def _():
            came(1, group, piece)
            total[...] += partial[1, group, piece].astype(jnp.float32)

        gained = total[...] * gain_ref[cols].astype(jnp.float32).reshape(1, tile)
        new_out[:, cols] = gained
        return slope + jnp.sum(
            gained * state_own[:, cols].astype(jnp.float32), axis=1, keepdims=True
        )

    slope = lax.fori_loop(0, pieces, last_piece, jnp.zeros((own, 1), jnp.float32))
    bend = inverse**3 * (slope / model)

    def update(piece, _):
        cols = pl.ds(pl.multiple_of(piece * tile, tile), tile)
        here = state_own[:, cols].astype(jnp.float32)
        gradient = readout_ref[:, cols] + inverse * new_out[:, cols] - here * bend
        new_out[:, cols] = (
            here - STEP_SIZE * gradient + NOISE_SCALE * noise_ref[:, cols].astype(jnp.float32)
        )
        return 0

    lax.fori_loop(0, pieces, update, 0)
    for order, dest in enumerate(dests):
        copies[order].wait_send()
        for step in range(1, ctx_count):
            exchange(order, dest, step).wait_send()
        if order < groups - 1:
            for piece in range(pieces):
                chain(order, dest, piece).wait_send()


def finish_step(
    ctx_count, head_count, query_grad, pair, w_qkv, w_pair, state, noise, readout, gain
):
    own, model = readout.shape
    width = w_qkv.shape[2]
    groups, pieces = head_count // 2, 4
    half, full, dma = jnp.bfloat16, jnp.float32, pltpu.SemaphoreType.DMA
    tile = model // pieces
    return pl.pallas_call(
        functools.partial(finish_kernel, ctx_count, head_count),
        out_shape=jax.ShapeDtypeStruct((own, model), full),
        in_specs=[VMEM, VMEM, ANY, ANY, ANY, VMEM, VMEM, VMEM],
        out_specs=VMEM,
        scratch_shapes=[
            pltpu.VMEM((2,) + w_qkv.shape, half),
            pltpu.VMEM((groups, ctx_count, own, 2 * HEAD_DIM), half),
            pltpu.VMEM((groups, ctx_count, 3, own, HEAD_DIM), half),
            pltpu.VMEM((groups, 2, 3, own, width), half),
            pltpu.VMEM((2, groups, pieces, own, tile), half),
            pltpu.VMEM((groups, pieces, own, tile), half),
            pltpu.VMEM((own, tile), full),
            pltpu.VMEM((own, model), half),
            dma((groups,)),
            dma((groups,)),
            dma((groups, ctx_count)),
            dma((groups, ctx_count)),
            dma((groups, pieces)),
            dma((2, groups, pieces)),
            dma((3,)),
        ],
        compiler_params=pltpu.CompilerParams(
            collective_id=2, has_side_effects=True, vmem_limit_bytes=60 * 2**20
        ),
    )(query_grad, pair, w_qkv, w_pair, state, noise, readout, gain)


def heads_body(state, norm_gain, w_qkv, w_out, probe, noise, segment_ids):
    rows, model = state.shape
    head_count, ctx_count = lax.axis_size("head"), lax.axis_size("ctx")
    own, groups = rows // head_count, head_count // 2
    queries, kv, segs, outputs, logs, grads_out, readout, w_pair = front(
        ctx_count, head_count, state, w_qkv, norm_gain, segment_ids, w_out, probe
    )
    mine, total = ctx_count * groups * own, ctx_count * rows
    parts, sub, bk = 1, groups * own, min(rows, 512)
    query_grad, pair = pl.pallas_call(
        functools.partial(head_backward_kernel, rows, own, parts, sub, bk),
        out_shape=(
            jax.ShapeDtypeStruct((mine, HEAD_DIM), jnp.bfloat16),
            jax.ShapeDtypeStruct((total, 2 * HEAD_DIM), jnp.bfloat16),
        ),
        in_specs=[VMEM] * 6,
        out_specs=(VMEM, VMEM),
        scratch_shapes=[pltpu.VMEM((total, 2 * HEAD_DIM), jnp.float32)],
        compiler_params=pltpu.CompilerParams(vmem_limit_bytes=60 * 2**20),
        cost_estimate=pl.CostEstimate(
            flops=10 * mine * total * HEAD_DIM, bytes_accessed=0, transcendentals=0
        ),
    )(
        segs, queries.reshape(mine, HEAD_DIM), kv.reshape(2, total, HEAD_DIM),
        grads_out.reshape(mine, HEAD_DIM), outputs.reshape(mine, HEAD_DIM), logs,
    )
    return finish_step(
        ctx_count, head_count, query_grad.reshape(ctx_count, groups, own, HEAD_DIM),
        pair.reshape(ctx_count, groups, 2, own, 2 * HEAD_DIM), w_qkv, w_pair, state, noise, readout,
        norm_gain,
    )


def solution(mesh):
    placed = (
        P("ctx", None),
        P(),
        P(None, None, "head"),
        P("head", None),
        P("ctx", None),
        P(("ctx", "head"), None),
        P("ctx"),
    )

    def step(*args):
        heads = args[2].shape[2] // HEAD_DIM
        return (heads_body if lax.axis_size("ctx") == 2 * heads == 4 else body)(*args)

    return jax.shard_map(
        step, mesh=mesh, in_specs=placed, out_specs=P(("ctx", "head"), None), check_vma=False
    )
```

profile of v0, /device:TPU:0, one launch (start us, length us, event | category | flops | bytes accessed | tf_op | source)
XLA Modules:
  0.0 153.3 jit_solution(4694414051678248448)
XLA Ops:
  0.0 71.8 %shard_map.73 = (bf16[4,512,128]{2,1,0:T(8,128)(2,1)}, bf16[2,4,1024,128]{3,2,1,0:T(8,128)(2,1)}, s32[4,8,128]{2,1,0:T(8,128)}, bf16[4,512,128]{2,1,0:T(8,128)(2...) custom-call(bf16[1024,2048]{1,0:T(8,128)(2,1)} %state_any.3, ...), custom_call_target="tpu_custom_call" | custom-call | tf_op jit(solution)/shard_map/pallas_call | solution.py:1189
  71.8 23.3 %shard_map.74 = (bf16[2048,128]{1,0:T(8,128)(2,1)}, bf16[4096,256]{1,0:T(8,128)(2,1)}) custom-call(s32[4,8,128]{2,1,0:T(8,128)} %get-tuple-element.15.segs_ref, bf16[2048,128]{1,0:T(8,128)(2,1)} %bitcast.11, bf16[2,4096,128]{2,1,0:T(8,128)(2,1)} %bitcast.10, bf16[2048,128]{1,0:T(8,128)(2,1)} %bitcast.13, bf16[2048,128]{1,0:T(8,128)(2,1)} %bitcast.12, ...), custom_call_target="tpu_custom_call" | custom-call | flops 10737418240 | tf_op jit(solution)/shard_map/pallas_call | solution.py:1575
  95.1 55.9 %shard_map.75 = f32[128,2048]{1,0:T(8,128)} custom-call(bf16[4,4,128,128]{3,2,1,0:T(8,128)(2,1)} %bitcast.8, bf16[4,4,2,128,256]{4,3,2,1,0:T(8,128)(2,1)} %bitcast.7, bf16[3,2048,256]{2,1,0:T(8,128)(2,1)} %w_any.3, bf16[3,2048,256]{2,1,0:T(8,128)(2,1)} %get-tuple-element.23.w_pair, bf16[1024,2048]{1,0:T(8,128)(2,1)} %state_any.3, ...), custom_call_target="tpu_custom_call" | custom-call | tf_op jit(solution)/shard_map/pallas_call | solution.py:1538
  151.0 2.3 %copy.9 = f32[128,2048]{1,0:T(8,128)} copy(f32[128,2048]{1,0:T(8,128)} %shard_map.75) | data formatting | bytes 2097152
where the time goes:
time: 151 us; the launch traced here: 153 us
  Pallas kernels  151 us (100%)
  local copies, waits for them, and re-layouts  2.3 us (2%)
    pallas_call x1, Pallas kernels, front(): pl.pallas_call(functools.partial(front_kernel, ctx_count, head_count), ou...  71.8 us
    pallas_call x1, Pallas kernels, finish_step(): pl.pallas_call(functools.partial(finish_kernel, ctx_count, head_count), o...  55.9 us
    pallas_call x1, Pallas kernels, heads_body(): pl.pallas_call(functools.partial(head_backward_kernel, rows, own, parts,...  23.3 us

commit v1 on v0

--- a/solution.py
+++ b/solution.py
@@ -641,11 +641,6 @@
     pl.semaphore_wait(pltpu.get_barrier_semaphore(), len(peers))
 
 
-def meet(peers):
-    announce(peers)
-    await_all(peers)
-
-
 def far_first(groups, group, step):
     result = 0
     for index in range(groups):
@@ -811,11 +806,11 @@
         head = group * 2 + kind
         return (
             remote(
-                query_buf.at[slot, piece, kind], query_out.at[ctx, own_at(piece)],
+                query_buf.at[slot, piece, kind], query_out.at[ctx, piece],
                 q_send.at[slot, kind, piece], q_recv.at[ctx, piece], dest, head,
             ),
             remote(
-                kv_buf.at[slot, kind, piece], kv_out.at[kind, ctx, at(piece)],
+                kv_buf.at[slot, kind, piece], kv_out.at[kind, ctx, piece],
                 kv_send.at[slot, kind, piece], kv_recv.at[kind, ctx, piece], dest, head,
             ),
         )
@@ -823,14 +818,14 @@
     def beside(slot, piece):
         result = [
             remote(
-                query_buf.at[slot, piece, 1 - core], query_out.at[ctx, own_at(piece)],
+                query_buf.at[slot, piece, 1 - core], query_out.at[ctx, piece],
                 q_send.at[slot, 1 - core, piece], q_recv.at[ctx, piece], ctx, partner,
             )
         ]
         for kind in range(2):
             result.append(
                 remote(
-                    kv_buf.at[slot, kind, piece], kv_out.at[kind, ctx, at(piece)],
+                    kv_buf.at[slot, kind, piece], kv_out.at[kind, ctx, piece],
                     kv_send.at[slot, kind, piece], kv_recv.at[kind, ctx, piece], ctx, partner,
                 )
             )
@@ -864,9 +859,9 @@
 
             @pl.when(dest == ctx)
             def _():
-                query_out[ctx, own_at(piece), :] = query_buf[slot, piece, core]
+                query_out[ctx, piece] = query_buf[slot, piece, core]
                 for kind in range(2):
-                    kv_out[kind, ctx, at(piece), :] = kv_buf[slot, kind, piece]
+                    kv_out[kind, ctx, piece] = kv_buf[slot, kind, piece]
                 for copy in beside(slot, piece):
                     copy.start()
 
@@ -895,7 +890,7 @@
     def hand_over(piece, step):
         source = lax.rem(ctx + step, ctx_count)
         return remote(
-            kv_out.at[core, source, at(piece)], kv_out.at[core, source, at(piece)],
+            kv_out.at[core, source, piece], kv_out.at[core, source, piece],
             pass_send.at[step, piece], kv_recv.at[core, source, piece], ctx, partner,
         )
 
@@ -912,13 +907,13 @@
 
     def got_query(source, piece):
         remote(
-            query_out.at[source, own_at(piece)], query_out.at[source, own_at(piece)],
+            query_out.at[source, piece], query_out.at[source, piece],
             q_send.at[0, 0, piece], q_recv.at[source, piece], ctx, partner,
         ).wait_recv()
 
     def got_kv(kind, source, piece):
         remote(
-            kv_out.at[kind, source, at(piece)], kv_out.at[kind, source, at(piece)],
+            kv_out.at[kind, source, piece], kv_out.at[kind, source, piece],
             kv_send.at[0, 0, piece], kv_recv.at[kind, source, piece], ctx, partner,
         ).wait_recv()
 
@@ -941,9 +936,17 @@
     for copy in segs:
         copy.wait()
     leaving = [
-        pltpu.make_async_copy(query_out, query_any, leave_sem.at[0]),
-        pltpu.make_async_copy(kv_out, kv_any, leave_sem.at[1]),
+        pltpu.make_async_copy(query_out.at[source], query_any.at[:, source], leave_sem.at[0, source])
+        for source in range(ctx_count)
     ]
+    for kind in range(2):
+        leaving += [
+            pltpu.make_async_copy(
+                kv_out.at[kind, source], kv_any.at[kind, :, source],
+                leave_sem.at[1 + kind, source],
+            )
+            for source in range(ctx_count)
+        ]
     for copy in leaving:
         copy.start()
     pair_copy = remote(w_any, w_pair, pair_send, pair_recv, ctx, partner)
@@ -970,12 +973,12 @@
 
     def out_copy(tile, order, other):
         return remote(
-            part_out.at[tile, own_at(other)], joined.at[:, cols_of(group, ctx)],
+            part_out.at[tile, other], joined.at[:, cols_of(group, ctx)],
             out_send.at[tile, order], out_recv.at[group, ctx], tile, other * 2 + core,
         )
 
     def one_tile(tile, _):
-        query = query_out[tile]
+        query = query_out[tile].reshape(sub, HEAD_DIM)
         pos = (tile * rows + inside).astype(jnp.float32)
         start = jnp.where(
             pos >= second_bound, second_bound, jnp.where(pos >= first_bound, first_bound, 0.0)
@@ -983,7 +986,7 @@
 
         def step(diagonal, piece, carry):
             top, total, acc = carry
-            scores = dot32(kv_out[0, piece], query, NT)
+            scores = dot32(kv_out[0, piece].reshape(rows, HEAD_DIM), query, NT)
             allowed = key_row >= start - piece * rows
             if diagonal:
                 allowed = allowed & (key_row <= inside)
@@ -992,7 +995,9 @@
             weights = jnp.exp2(scores * factor - new_top)
             scale = jnp.exp2(top - new_top)
             total = total * scale + jnp.sum(weights, axis=0, keepdims=True)
-            acc = acc * scale + dot32(kv_out[1, piece], weights.astype(jnp.bfloat16), TN)
+            acc = acc * scale + dot32(
+                kv_out[1, piece].reshape(rows, HEAD_DIM), weights.astype(jnp.bfloat16), TN
+            )
             return new_top, total, acc
 
         carry = (
@@ -1002,8 +1007,10 @@
         )
         carry = lax.fori_loop(0, tile, functools.partial(step, False), carry)
         top, total, acc = step(True, tile, carry)
-        part_out[tile] = (acc / total).T.astype(jnp.bfloat16)
-        log_out[tile] = top + jnp.log2(total)
+        part_out[tile] = (acc / total).T.astype(jnp.bfloat16).reshape(groups, own, HEAD_DIM)
+        log_row = top + jnp.log2(total)
+        for index in range(groups):
+            log_out[index, :, own_at(tile)] = log_row[:, index * own : (index + 1) * own]
         for order in range(groups):
             other = far_first(groups, group, order)
             if order == groups - 1:
@@ -1014,7 +1021,7 @@
 
                 @pl.when(tile == ctx)
                 def _():
-                    joined[:, cols_of(group, ctx)] = part_out[tile, own_at(group), :]
+                    joined[:, cols_of(group, ctx)] = part_out[tile, group]
 
             else:
                 out_copy(tile, order, other).start()
@@ -1026,8 +1033,13 @@
         return 0
 
     lax.fori_loop(0, ctx_count, one_tile, 0)
-    leaving.append(pltpu.make_async_copy(part_out, part_any, leave_sem.at[2]))
-    leaving[-1].start()
+    for source in range(ctx_count):
+        leaving.append(
+            pltpu.make_async_copy(
+                part_out.at[source], part_any.at[:, source], leave_sem.at[3, source]
+            )
+        )
+        leaving[-1].start()
     for copy in later_loads:
         copy.wait()
     sources = []
@@ -1057,7 +1069,7 @@
             if order < groups - 1 or step:
                 peer = lax.rem(ctx + step, ctx_count)
                 remote(
-                    part_out.at[0, own_at(0)], joined.at[:, cols_of(other, peer)],
+                    part_out.at[0, 0], joined.at[:, cols_of(other, peer)],
                     out_send.at[0, 0], out_recv.at[other, peer], peer, other * 2 + core,
                 ).wait_recv()
 
@@ -1105,7 +1117,7 @@
         return 0
 
     lax.fori_loop(0, model // tile, finish, 0)
-    leaving.append(pltpu.make_async_copy(readout_out, readout_any, leave_sem.at[3]))
+    leaving.append(pltpu.make_async_copy(readout_out, readout_any, leave_sem.at[4, 0]))
     leaving[-1].start()
     copies = []
     for order in range(groups):
@@ -1120,12 +1132,12 @@
             if order == groups - 1 and step == 0:
                 continue
             copy = remote(
-                sending.at[order, peer], grad_out.at[ctx, group], back_send.at[order, step],
+                sending.at[order, peer], grad_out.at[group, ctx], back_send.at[order, step],
                 back_recv.at[ctx, group], peer, other * 2 + core,
             )
             copy.start()
             copies.append(copy)
-    last = pltpu.make_async_copy(sending.at[groups - 1, ctx], grad_out.at[ctx, group], own_sem)
+    last = pltpu.make_async_copy(sending.at[groups - 1, ctx], grad_out.at[group, ctx], own_sem)
     last.start()
 
     def sent(piece, _):
@@ -1168,7 +1180,7 @@
     lax.fori_loop(0, ctx_count, parts_sent, 0)
     for other, peer in sources:
         remote(
-            sending.at[0, 0], grad_out.at[peer, other], back_send.at[0, 0],
+            sending.at[0, 0], grad_out.at[other, peer], back_send.at[0, 0],
             back_recv.at[peer, other], peer, other * 2 + core,
         ).wait_recv()
     for copy in copies:
@@ -1189,12 +1201,12 @@
     return pl.pallas_call(
         functools.partial(front_kernel, ctx_count, head_count),
         out_shape=(
-            shape((ctx_count, groups * own, HEAD_DIM), half),
-            shape((2, ctx_count, rows, HEAD_DIM), half),
+            shape((groups, ctx_count, own, HEAD_DIM), half),
+            shape((2, groups, ctx_count, 2 * own, HEAD_DIM), half),
             shape((ctx_count,) + seg.shape, seg.dtype),
-            shape((ctx_count, groups * own, HEAD_DIM), half),
-            shape((ctx_count, 1, groups * own), full),
-            shape((ctx_count, groups, own, HEAD_DIM), half),
+            shape((groups, ctx_count, own, HEAD_DIM), half),
+            shape((groups, 1, ctx_count * own), full),
+            shape((groups, ctx_count, own, HEAD_DIM), half),
             shape((own, model), full),
             shape(w_qkv.shape, half),
         ),
@@ -1211,9 +1223,9 @@
             pltpu.VMEM((groups, ctx_count, own, HEAD_DIM), half),
             pltpu.VMEM((own, model), half),
             pltpu.VMEM((own, model), half),
-            pltpu.VMEM((ctx_count, groups * own, HEAD_DIM), half),
-            pltpu.VMEM((2, ctx_count, rows, HEAD_DIM), half),
-            pltpu.VMEM((ctx_count, groups * own, HEAD_DIM), half),
+            pltpu.VMEM((ctx_count, groups, own, HEAD_DIM), half),
+            pltpu.VMEM((2, ctx_count, groups, 2 * own, HEAD_DIM), half),
+            pltpu.VMEM((ctx_count, groups, own, HEAD_DIM), half),
             pltpu.VMEM((own, model), full),
             dma((groups,)),
             dma((3,)),
@@ -1241,7 +1253,7 @@
             dma((2,)),
             dma,
             dma,
-            dma((4,)),
+            dma((5, ctx_count)),
         ],
         compiler_params=pltpu.CompilerParams(
             collective_id=0, has_side_effects=True, vmem_limit_bytes=62 * 2**20
@@ -1249,158 +1261,157 @@
     )(state, w_qkv, gain, seg, w_out, probe)
 
 
-def segment_bounds(segs_ref):
-    segs = segs_ref[...]
-
-    def below(value):
-        return jnp.sum(jnp.where(segs < value, 1.0, 0.0)).astype(jnp.int32)
-
-    return below(1), below(2)
-
-
-def tile_plan(bounds, rows, own, parts, sub, bk, tile, core):
-    first_bound, second_bound = bounds
-
-    def start_of(pos):
-        return jnp.where(pos >= second_bound, second_bound, jnp.where(pos >= first_bound, first_bound, 0))
-
-    blocks = sub // own
-    base = tile * rows + core * own
-    places = []
-    for part in range(parts):
-        lane = lax.broadcasted_iota(jnp.int32, (1, sub), 1)
-        pos = base + (lane // own + part * blocks) * (2 * own) + lane % own
-        places.append((start_of(pos), pos))
-    first, last = base, base + (parts * blocks - 1) * 2 * own + own - 1
-    low = start_of(first) // bk
-    inner_low = (start_of(last) + bk - 1) // bk
-    inner_high = jnp.maximum(inner_low, (first + 1) // bk)
-    high = last // bk + 1
-    return places, low, inner_low, inner_high, high
-
-
-def head_backward_kernel(
-    rows, own, parts, sub, bk, segs_ref, query_ref, kv_ref, grad_ref, out_ref, log_ref, query_out,
-    pair_out, pair_acc,
-):
-    score_scale = HEAD_DIM ** (-0.5)
-    factor = score_scale * LOG2E
-    core = lax.rem(lax.axis_index("head"), 2)
-    bounds = segment_bounds(segs_ref)
-    tiles = query_ref.shape[0] // (parts * sub)
-    pair_rows = pair_acc.shape[0]
-
-    def clear(piece, _):
-        at = pl.ds(pl.multiple_of(piece * bk, bk), bk)
-        pair_acc[at, :] = jnp.zeros((bk, 2 * HEAD_DIM), jnp.float32)
-        return 0
-
-    lax.fori_loop(0, pair_rows // bk, clear, 0)
-
-    def one_tile(tile, _):
-        places, low, inner_low, inner_high, high = tile_plan(
-            bounds, rows, own, parts, sub, bk, tile, core
-        )
-
-        def at(part):
-            return pl.ds(pl.multiple_of((tile * parts + part) * sub, sub), sub)
-
-        deltas, logs = [], []
-        for part in range(parts):
-            product = grad_ref[at(part), :].astype(jnp.float32) * out_ref[at(part), :].astype(
-                jnp.float32
-            )
-            deltas.append(jnp.sum(product.T, axis=0, keepdims=True))
-            logs.append(log_ref[tile, pl.ds(part, 1), :])
-
-        def step(masked, piece, carry):
-            keys_at = pl.ds(pl.multiple_of(piece * bk, bk), bk)
-            if masked:
-                key_pos = piece * bk + lax.broadcasted_iota(jnp.int32, (bk, sub), 0)
-            result = []
-            key_block, value_block = kv_ref[0, keys_at, :], kv_ref[1, keys_at, :]
-            for part in range(parts):
-                query_block, grad_block = query_ref[at(part), :], grad_ref[at(part), :]
-                scores = dot32(key_block, query_block, NT)
-                probabilities = jnp.exp2(scores * factor - logs[part])
-                if masked:
-                    start, pos = places[part]
-                    probabilities = jnp.where(
-                        (key_pos >= start) & (key_pos <= pos), probabilities, 0.0
-                    )
-                dprobs = dot32(value_block, grad_block, NT)
-                dscores = (probabilities * (dprobs - deltas[part])).astype(jnp.bfloat16)
-                pair_acc[keys_at, HEAD_DIM:] += jnp.dot(
-                    probabilities.astype(jnp.bfloat16),
-                    grad_block,
-                    preferred_element_type=jnp.float32,
-                )
-                pair_acc[keys_at, :HEAD_DIM] += jnp.dot(
-                    dscores, query_block, preferred_element_type=jnp.float32
-                )
-                result.append(carry[part] + dot32(key_block, dscores, TN))
-            return tuple(result)
-
-        carry = tuple(jnp.zeros((HEAD_DIM, sub), jnp.float32) for _ in range(parts))
-        carry = lax.fori_loop(low, inner_low, functools.partial(step, True), carry)
-        carry = lax.fori_loop(inner_low, inner_high, functools.partial(step, False), carry)
-        carry = lax.fori_loop(inner_high, high, functools.partial(step, True), carry)
-        for part in range(parts):
-            query_out[at(part), :] = (carry[part].T * score_scale).astype(jnp.bfloat16)
-        return 0
-
-    lax.fori_loop(0, tiles, one_tile, 0)
-
-    def flush(piece, _):
-        at = pl.ds(pl.multiple_of(piece * bk, bk), bk)
-        pair_out[at, :HEAD_DIM] = (pair_acc[at, :HEAD_DIM] * score_scale).astype(jnp.bfloat16)
-        pair_out[at, HEAD_DIM:] = pair_acc[at, HEAD_DIM:].astype(jnp.bfloat16)
-        return 0
-
-    lax.fori_loop(0, pair_rows // bk, flush, 0)
-
-
-def finish_kernel(
-    ctx_count, head_count, query_ref, pair_ref, w_any, w_pair, state_any, noise_ref, readout_ref,
-    gain_ref, new_out, w_both, beside, away, terms_in, partial, sending, total, state_own, b_send,
-    b_recv, a_send, a_recv, z_send, z_recv, own_sem,
+def back_kernel(
+    ctx_count, head_count, query_any, kv_any, grad_any, part_any, segs_ref, log_ref, w_any, w_pair,
+    state_any, noise_any, readout_any, gain_ref, new_out, query_v, kv_v, grad_v, part_v, pair_acc,
+    query_acc, deltas, query_fin, pair_buf, w_both, beside, away, terms_in, partial, sending, total,
+    state_own, noise_own, readout_own, in_sem, b_send, b_recv, a_send, a_recv, z_send, z_recv,
+    own_sem,
 ):
     ctx, me, group, core = place()
     groups = head_count // 2
     own, model = new_out.shape
-    slots = ctx_count // 2
+    slots, halves = ctx_count // 2, 2
+    rows = groups * 2 * own
+    sub = ctx_count * own // halves
     partner = group * 2 + 1 - core
     my_rows = pl.ds(pl.multiple_of(me * own, own), own)
+    inputs = [
+        pltpu.make_async_copy(source, target, in_sem.at[index])
+        for index, (source, target) in enumerate(
+            ((grad_any, grad_v), (part_any, part_v), (query_any, query_v), (kv_any, kv_v))
+        )
+    ]
     loads = [
         pltpu.make_async_copy(w_any, w_both.at[core], own_sem.at[0]),
         pltpu.make_async_copy(w_pair, w_both.at[1 - core], own_sem.at[1]),
         pltpu.make_async_copy(state_any.at[my_rows], state_own, own_sem.at[2]),
+        pltpu.make_async_copy(noise_any, noise_own, own_sem.at[3]),
+        pltpu.make_async_copy(readout_any, readout_own, own_sem.at[4]),
     ]
-    for copy in loads:
+    for copy in inputs:
         copy.start()
     peers = [(ctx, partner)]
     peers += [(lax.rem(ctx + step, ctx_count), me) for step in range(1, ctx_count)]
     peers += [(ctx, lax.rem(group + far, groups) * 2 + core) for far in range(1, groups)]
-    meet(peers)
+    announce(peers)
     dests = [far_first(groups, group, order) for order in range(groups)]
-    copies = []
-    for order, dest in enumerate(dests):
-        copy = remote(
-            pair_ref.at[:, dest, 1 - core], beside.at[order], b_send.at[order], b_recv.at[order],
-            ctx, partner,
-        )
+
+    def dest_of(order):
+        result = dests[0]
+        for index in range(1, groups):
+            result = jnp.where(order == index, dests[index], result)
+        return result
+
+    score_scale = HEAD_DIM ** (-0.5)
+    factor = score_scale * LOG2E
+    seg_all = segs_ref[...]
+
+    def below(value):
+        count = jnp.where(seg_all < value, 1.0, 0.0)
+        for axis in (0, 1, 2):
+            count = jnp.sum(count, axis=axis, keepdims=True)
+        return count[0]
+
+    first_bound, second_bound = below(1), below(2)
+
+    def clear(index, _):
+        pair_acc[index] = jnp.zeros(pair_acc.shape[1:], jnp.float32)
+        query_acc[index] = jnp.zeros(query_acc.shape[1:], jnp.float32)
+        return 0
+
+    lax.fori_loop(0, groups, clear, 0)
+    for copy in inputs:
+        copy.wait()
+    for copy in loads:
         copy.start()
-        copies.append(copy)
+
+    def half_of(ref, index, half):
+        count = ctx_count // halves
+        return ref[index, half * count : (half + 1) * count].reshape(sub, HEAD_DIM)
+
+    def find_deltas(index, _):
+        for half in range(halves):
+            product = half_of(grad_v, index, half).astype(jnp.float32) * half_of(
+                part_v, index, half
+            ).astype(jnp.float32)
+            deltas[index, :, half * sub : (half + 1) * sub] = jnp.sum(
+                product.T, axis=0, keepdims=True
+            )
+        return 0
+
+    lax.fori_loop(0, groups, find_deltas, 0)
+    await_all(peers)
+    lane = lax.broadcasted_iota(jnp.int32, (1, sub), 1)
+
+    def pair(query_at, key_at):
+        for half in range(halves):
+            blocks = (half + 1) * ctx_count // halves
+            count = blocks * 2 * own
+            lanes = slice(half * sub, (half + 1) * sub)
+            key_block = kv_v[0, key_at, :blocks].reshape(count, HEAD_DIM)
+            value_block = kv_v[1, key_at, :blocks].reshape(count, HEAD_DIM)
+            query_block = half_of(query_v, query_at, half)
+            grad_block = half_of(grad_v, query_at, half)
+            spot = (half * (ctx_count // halves) + lane // own) * rows + lane % own
+            pos = spot + (query_at * 2 + core) * own
+            pos_f = pos.astype(jnp.float32)
+            start = jnp.where(
+                pos_f >= second_bound,
+                second_bound,
+                jnp.where(pos_f >= first_bound, first_bound, 0.0),
+            ).astype(jnp.int32)
+            line = lax.broadcasted_iota(jnp.int32, (count, sub), 0)
+            key_pos = (line // (2 * own)) * rows + line % (2 * own)
+            offset = key_at * 2 * own
+            allowed = (key_pos >= start - offset) & (key_pos <= pos - offset)
+            scores = dot32(key_block, query_block, NT)
+            probabilities = jnp.where(
+                allowed, jnp.exp2(scores * factor - log_ref[query_at, :, lanes]), 0.0
+            )
+            dprobs = dot32(value_block, grad_block, NT)
+            dscores = (probabilities * (dprobs - deltas[query_at, :, lanes])).astype(jnp.bfloat16)
+            pair_acc[key_at, :count, HEAD_DIM:] += jnp.dot(
+                probabilities.astype(jnp.bfloat16), grad_block, preferred_element_type=jnp.float32
+            )
+            pair_acc[key_at, :count, :HEAD_DIM] += jnp.dot(
+                dscores, query_block, preferred_element_type=jnp.float32
+            )
+            query_acc[query_at, :, lanes] += dot32(key_block, dscores, TN)
+
+    def beside_copy(order):
+        return remote(
+            pair_buf.at[order], beside.at[order], b_send.at[order], b_recv.at[order], ctx, partner
+        )
+
+    def pair_rows(dest, source, kind):
+        first = pl.multiple_of((source * 2 + kind) * own, own)
+        keys = pair_acc[dest, pl.ds(first, own), :HEAD_DIM] * score_scale
+        values = pair_acc[dest, pl.ds(first, own), HEAD_DIM:]
+        return keys, values
+
+    def settle(order):
+        dest = dest_of(order)
+        for source in range(ctx_count):
+            keys, values = pair_rows(dest, source, 1 - core)
+            pair_buf[order, source, :, :HEAD_DIM] = keys.astype(jnp.bfloat16)
+            pair_buf[order, source, :, HEAD_DIM:] = values.astype(jnp.bfloat16)
+        for half in range(halves):
+            query_fin[order, half * sub : (half + 1) * sub, :] = (
+                query_acc[dest, :, half * sub : (half + 1) * sub].T * score_scale
+            ).astype(jnp.bfloat16)
+        beside_copy(order).start()
 
     def stripe(source):
         slot = lax.rem(source, slots)
         return pl.ds(pl.multiple_of(slot * HEAD_DIM, HEAD_DIM), HEAD_DIM)
 
-    def exchange(order, dest, step):
+    def exchange(order, step):
         peer = lax.rem(ctx + step, ctx_count)
         return remote(
-            away.at[order, step], terms_in.at[dest, ctx // slots, :, :, stripe(ctx)],
-            a_send.at[order, step], a_recv.at[dest, ctx], peer, me,
+            away.at[order, step],
+            terms_in.at[dest_of(order), ctx // slots, :, :, stripe(ctx)],
+            a_send.at[order, step], a_recv.at[dest_of(order), ctx], peer, me,
         )
 
     def arrived(dest, step):
@@ -1410,32 +1421,35 @@
             a_send.at[0, 0], a_recv.at[dest, source], source, me,
         ).wait_recv()
 
-    for order, dest in enumerate(dests):
-        copies[order].wait_recv()
-        for step in range(1, ctx_count):
+    def spread(order):
+        dest = dest_of(order)
+        beside_copy(order).wait_recv()
+        for step in range(1, ctx_count + 1):
             peer = lax.rem(ctx + step, ctx_count)
-            pair = pair_ref[peer, dest, core].astype(jnp.float32) + beside[order, peer].astype(
-                jnp.float32
+            keys, values = pair_rows(dest, peer, core)
+            keys = (keys + beside[order, peer, :, :HEAD_DIM].astype(jnp.float32)).astype(
+                jnp.bfloat16
             )
-            pair = pair.astype(jnp.bfloat16)
-            away[order, step, 0] = query_ref[peer, dest]
-            away[order, step, 1] = pair[:, :HEAD_DIM]
-            away[order, step, 2] = pair[:, HEAD_DIM:]
-            exchange(order, dest, step).start()
-        pair = pair_ref[ctx, dest, core].astype(jnp.float32) + beside[order, ctx].astype(
-            jnp.float32
-        )
-        pair = pair.astype(jnp.bfloat16)
-        at = stripe(ctx)
-        terms_in[dest, ctx // slots, 0, :, at] = query_ref[ctx, dest]
-        terms_in[dest, ctx // slots, 1, :, at] = pair[:, :HEAD_DIM]
-        terms_in[dest, ctx // slots, 2, :, at] = pair[:, HEAD_DIM:]
-    for copy in loads:
-        copy.wait()
+            values = (values + beside[order, peer, :, HEAD_DIM:].astype(jnp.float32)).astype(
+                jnp.bfloat16
+            )
+            queries = query_fin[order, pl.ds(pl.multiple_of(peer * own, own), own), :]
+            if step < ctx_count:
+                away[order, step, 0] = queries
+                away[order, step, 1] = keys
+                away[order, step, 2] = values
+                exchange(order, step).start()
+            else:
+                at = stripe(ctx)
+                terms_in[dest, ctx // slots, 0, :, at] = queries
+                terms_in[dest, ctx // slots, 1, :, at] = keys
+                terms_in[dest, ctx // slots, 2, :, at] = values
+
     pieces = partial.shape[2]
     tile = model // pieces
 
-    def chain(order, dest, piece):
+    def chain(order, piece):
+        dest = dest_of(order)
         up = dest > group
         line = jnp.where(up, 0, 1)
         peer = jnp.where(up, group + 1, group - 1)
@@ -1459,11 +1473,13 @@
                 result = part if result is None else result + part
         return result
 
-    for order, dest in enumerate(dests[:-1]):
+    inner = (group > 0) & (group < groups - 1)
+
+    def pass_on(order, _):
+        dest = dest_of(order)
         for step in range(1, ctx_count):
             arrived(dest, step)
         line = jnp.where(dest > group, 0, 1)
-        inner = (group > 0) & (group < groups - 1)
 
         def one_piece(piece, _):
             total[...] = term(dest, piece)
@@ -1474,11 +1490,62 @@
                 total[...] += partial[line, dest, piece].astype(jnp.float32)
 
             sending[order, piece] = total[...].astype(jnp.bfloat16)
-            chain(order, dest, piece).start()
+            chain(order, piece).start()
             return 0
 
         lax.fori_loop(0, pieces, one_piece, 0)
-
+        return 0
+
+    ends, number = [], 0
+    for order in range(groups):
+        number += 2 * (groups - order) - 1
+        ends.append(number - 1)
+    spreads = {order: end + 1 for order, end in enumerate(ends) if end + 1 < number}
+
+    def one_pair(index, _):
+        stage = 0
+        for end in ends[:-1]:
+            stage = stage + jnp.where(index > end, 1, 0)
+        first = 0
+        for order in range(1, groups):
+            first = jnp.where(stage == order, ends[order - 1] + 1, first)
+        inside = index - first
+        other = stage + (inside + 1) // 2
+        odd = lax.rem(inside, 2)
+        pair(
+            dest_of(jnp.where(odd == 1, stage, other)), dest_of(jnp.where(odd == 1, other, stage))
+        )
+        for order, end in enumerate(ends[:-1]):
+
+            @pl.when(index == end)
+            def _():
+                settle(order)
+
+        for order, at in spreads.items():
+
+            @pl.when(index == at)
+            def _():
+                spread(order)
+
+        return 0
+
+    first = min(ends[min(1, groups - 1)] + 2, number)
+    lax.fori_loop(0, first, one_pair, 0)
+    for copy in loads:
+        copy.wait()
+    early = 1 if first < number else 0
+    if early:
+
+        @pl.when(jnp.logical_not(inner))
+        def _():
+            pass_on(0, 0)
+
+        lax.fori_loop(first, number, one_pair, 0)
+    settle(groups - 1)
+    for order in range(groups):
+        if order not in spreads:
+            spread(order)
+    lax.fori_loop(jnp.where(inner, 0, early), groups - 1, pass_on, 0)
     for step in range(1, ctx_count):
         arrived(group, step)
 
@@ -1511,36 +1578,53 @@
     def update(piece, _):
         cols = pl.ds(pl.multiple_of(piece * tile, tile), tile)
         here = state_own[:, cols].astype(jnp.float32)
-        gradient = readout_ref[:, cols] + inverse * new_out[:, cols] - here * bend
+        gradient = readout_own[:, cols] + inverse * new_out[:, cols] - here * bend
         new_out[:, cols] = (
-            here - STEP_SIZE * gradient + NOISE_SCALE * noise_ref[:, cols].astype(jnp.float32)
+            here - STEP_SIZE * gradient + NOISE_SCALE * noise_own[:, cols].astype(jnp.float32)
         )
         return 0
 
     lax.fori_loop(0, pieces, update, 0)
-    for order, dest in enumerate(dests):
-        copies[order].wait_send()
+
+    def sent(order, _):
+        beside_copy(order).wait_send()
         for step in range(1, ctx_count):
-            exchange(order, dest, step).wait_send()
-        if order < groups - 1:
+            exchange(order, step).wait_send()
+
+        @pl.when(order < groups - 1)
+        def _():
             for piece in range(pieces):
-                chain(order, dest, piece).wait_send()
-
-
-def finish_step(
-    ctx_count, head_count, query_grad, pair, w_qkv, w_pair, state, noise, readout, gain
+                chain(order, piece).wait_send()
+
+        return 0
+
+    lax.fori_loop(0, groups, sent, 0)
+
+
+def back(
+    ctx_count, head_count, queries, kv, grads, parts, segs, logs, w_qkv, w_pair, state, noise,
+    readout, gain,
 ):
     own, model = readout.shape
     width = w_qkv.shape[2]
     groups, pieces = head_count // 2, 4
     half, full, dma = jnp.bfloat16, jnp.float32, pltpu.SemaphoreType.DMA
-    tile = model // pieces
+    tile, lanes = model // pieces, ctx_count * own
     return pl.pallas_call(
-        functools.partial(finish_kernel, ctx_count, head_count),
+        functools.partial(back_kernel, ctx_count, head_count),
         out_shape=jax.ShapeDtypeStruct((own, model), full),
-        in_specs=[VMEM, VMEM, ANY, ANY, ANY, VMEM, VMEM, VMEM],
+        in_specs=[ANY] * 4 + [VMEM] * 2 + [ANY] * 5 + [VMEM],
         out_specs=VMEM,
         scratch_shapes=[
+            pltpu.VMEM(queries.shape, half),
+            pltpu.VMEM(kv.shape, half),
+            pltpu.VMEM(queries.shape, half),
+            pltpu.VMEM(queries.shape, half),
+            pltpu.VMEM((groups, 2 * lanes, 2 * HEAD_DIM), full),
+            pltpu.VMEM((groups, HEAD_DIM, lanes), full),
+            pltpu.VMEM((groups, 1, lanes), full),
+            pltpu.VMEM((groups, lanes, HEAD_DIM), half),
+            pltpu.VMEM((groups, ctx_count, own, 2 * HEAD_DIM), half),
             pltpu.VMEM((2,) + w_qkv.shape, half),
             pltpu.VMEM((groups, ctx_count, own, 2 * HEAD_DIM), half),
             pltpu.VMEM((groups, ctx_count, 3, own, HEAD_DIM), half),
@@ -1549,50 +1633,33 @@
             pltpu.VMEM((groups, pieces, own, tile), half),
             pltpu.VMEM((own, tile), full),
             pltpu.VMEM((own, model), half),
+            pltpu.VMEM((own, model), half),
+            pltpu.VMEM((own, model), full),
+            dma((4,)),
             dma((groups,)),
             dma((groups,)),
             dma((groups, ctx_count)),
             dma((groups, ctx_count)),
             dma((groups, pieces)),
             dma((2, groups, pieces)),
-            dma((3,)),
+            dma((5,)),
         ],
         compiler_params=pltpu.CompilerParams(
-            collective_id=2, has_side_effects=True, vmem_limit_bytes=60 * 2**20
+            collective_id=2, has_side_effects=True, vmem_limit_bytes=62 * 2**20
         ),
-    )(query_grad, pair, w_qkv, w_pair, state, noise, readout, gain)
+    )(
+        queries, kv, grads, parts, segs, logs, w_qkv, w_pair, state, noise, readout, gain,
+    )
 
 
 def heads_body(state, norm_gain, w_qkv, w_out, probe, noise, segment_ids):
-    rows, model = state.shape
     head_count, ctx_count = lax.axis_size("head"), lax.axis_size("ctx")
-    own, groups = rows // head_count, head_count // 2
-    queries, kv, segs, outputs, logs, grads_out, readout, w_pair = front(
+    queries, kv, segs, parts, logs, grads, readout, w_pair = front(
         ctx_count, head_count, state, w_qkv, norm_gain, segment_ids, w_out, probe
     )
-    mine, total = ctx_count * groups * own, ctx_count * rows
-    parts, sub, bk = 1, groups * own, min(rows, 512)
-    query_grad, pair = pl.pallas_call(
-        functools.partial(head_backward_kernel, rows, own, parts, sub, bk),
-        out_shape=(
-            jax.ShapeDtypeStruct((mine, HEAD_DIM), jnp.bfloat16),
-            jax.ShapeDtypeStruct((total, 2 * HEAD_DIM), jnp.bfloat16),
-        ),
-        in_specs=[VMEM] * 6,
-        out_specs=(VMEM, VMEM),
-        scratch_shapes=[pltpu.VMEM((total, 2 * HEAD_DIM), jnp.float32)],
-        compiler_params=pltpu.CompilerParams(vmem_limit_bytes=60 * 2**20),
-        cost_estimate=pl.CostEstimate(
-            flops=10 * mine * total * HEAD_DIM, bytes_accessed=0, transcendentals=0
-        ),
-    )(
-        segs, queries.reshape(mine, HEAD_DIM), kv.reshape(2, total, HEAD_DIM),
-        grads_out.reshape(mine, HEAD_DIM), outputs.reshape(mine, HEAD_DIM), logs,
-    )
-    return finish_step(
-        ctx_count, head_count, query_grad.reshape(ctx_count, groups, own, HEAD_DIM),
-        pair.reshape(ctx_count, groups, 2, own, 2 * HEAD_DIM), w_qkv, w_pair, state, noise, readout,
-        norm_gain,
+    return back(
+        ctx_count, head_count, queries, kv, grads, parts, segs, logs, w_qkv, w_pair, state, noise,
+        readout, norm_gain,
     )
 
 

time: 151 us -> 141 us (0.934); the launches traced: 153 us -> 140 us
  Pallas kernels: 151 us -> 138 us
    pallas_call x2 -> x1, Pallas kernels: 79.2 us -> 66.1 us  [back(): pl.pallas_call(functools.partial(back_kernel, ctx_count, head_count), out...]
where the time goes in v1:
time: 141 us; the launch traced here: 140 us
  Pallas kernels  138 us (98%)
  local copies, waits for them, and re-layouts  2.3 us (2%)
    pallas_call x1, Pallas kernels, front(): pl.pallas_call(functools.partial(front_kernel, ctx_count, head_count), ou...  72 us
    pallas_call x1, Pallas kernels, back(): pl.pallas_call(functools.partial(back_kernel, ctx_count, head_count), out...  66.1 us

profile of v1, /device:TPU:0, one launch (start us, length us, event | category | flops | bytes accessed | tf_op | source)
XLA Modules:
  0.0 140.3 jit_solution(6141456931470654973)
XLA Ops:
  0.0 72.0 %shard_map.73 = (bf16[4,4,128,128]{3,2,1,0:T(8,128)(2,1)}, bf16[2,4,4,256,128]{4,3,2,1,0:T(8,128)(2,1)}, s32[4,8,128]{2,1,0:T(8,128)}, bf16[4,4,128,128]{3,2,1,0...) custom-call(bf16[1024,2048]{1,0:T(8,128)(2,1)} %state_any.3, ...), custom_call_target="tpu_custom_call" | custom-call | tf_op jit(solution)/shard_map/pallas_call | solution.py:1201
  72.0 66.1 %shard_map.74 = f32[128,2048]{1,0:T(8,128)} custom-call(bf16[4,4,128,128]{3,2,1,0:T(8,128)(2,1)} %get-tuple-element.13.query_any, bf16[2,4,4,256,128]{4,3,2,1,0:T(8,128)(2,1)} %get-tuple-element.14.kv_any, bf16[4,4,128,128]{3,2,1,0:T(8,128)(2,1)} %get-tuple-element.15.grad_any, bf16[4,4,128,128]{3,2,1,0:T(8,128)(2,1)} %get-tuple-element.16.part_any, ...), custom_call_target="tpu_custom_call" | custom-call | tf_op jit(solution)/shard_map/pallas_call | solution.py:1613
  138.0 2.3 %copy.9 = f32[128,2048]{1,0:T(8,128)} copy(f32[128,2048]{1,0:T(8,128)} %shard_map.74) | data formatting | bytes 2097152

commit v2 on v1

--- a/solution.py
+++ b/solution.py
@@ -649,14 +649,15 @@
     return result
 
 
-def front_kernel(
-    ctx_count, head_count, state_any, w_any, gain_ref, seg_ref, w_out_any, probe_any, query_any,
-    kv_any, segs_out, part_any, log_out, grad_out, readout_any, w_pair, state_v, w_v, query_buf,
-    kv_buf, w_ref, joined, half, sending, state_own, probe_own, query_out, kv_out, part_out,
-    readout_out, load_sem, w_sem, q_send, q_recv, kv_send, kv_recv, pass_send, seg_send, seg_recv,
-    line_send, line_recv, plane_send, plane_recv, beside_send, beside_recv, shard_send, shard_recv,
-    shard_sem, out_send, out_recv, back_send, back_recv, own_sem, row_sem, pair_send, pair_recv,
-    leave_sem,
+def step_kernel(
+    ctx_count, head_count, state_any, w_any, gain_ref, seg_ref, w_out_any, probe_any, noise_any,
+    new_out, state_v, query_buf, kv_buf, w_ref, joined, half, sending, state_own, probe_own,
+    noise_own, query_out, kv_out, part_out, readout_out, segs_out, log_v, grad_v, w_both, pair_acc,
+    query_acc, deltas, query_fin, pair_buf, beside_in, away_buf, terms_in, partial, passing, sum_v,
+    load_sem, w_sem, q_send, q_recv, kv_send, kv_recv, pass_send, seg_send, seg_recv, line_send,
+    line_recv, plane_send, plane_recv, beside_send, beside_recv, shard_send, shard_recv, shard_sem,
+    out_send, out_recv, back_send, back_recv, row_sem, pair_send, pair_recv, b_send, b_recv, a_send,
+    a_recv, z_send, z_recv,
 ):
     ctx, me, group, core = place()
     rows, model = state_any.shape
@@ -677,7 +678,9 @@
         )
 
     load_state(0).start()
-    w_loads = [pltpu.make_async_copy(w_any.at[t], w_v.at[t], w_sem.at[t]) for t in range(3)]
+    w_loads = [
+        pltpu.make_async_copy(w_any.at[t], w_both.at[core, t], w_sem.at[t]) for t in range(3)
+    ]
     for copy in w_loads:
         copy.start()
     for piece in range(1, groups):
@@ -688,6 +691,7 @@
     later_loads = [
         pltpu.make_async_copy(state_any.at[my_rows], state_own, row_sem.at[0]),
         pltpu.make_async_copy(probe_any.at[my_rows], probe_own, row_sem.at[1]),
+        pltpu.make_async_copy(noise_any, noise_own, row_sem.at[2]),
         pltpu.make_async_copy(
             w_out_any, w_ref.at[pl.ds(pl.multiple_of(me * shard, shard), shard)], shard_sem
         ),
@@ -806,11 +810,11 @@
         head = group * 2 + kind
         return (
             remote(
-                query_buf.at[slot, piece, kind], query_out.at[ctx, piece],
+                query_buf.at[slot, piece, kind], query_out.at[piece, ctx],
                 q_send.at[slot, kind, piece], q_recv.at[ctx, piece], dest, head,
             ),
             remote(
-                kv_buf.at[slot, kind, piece], kv_out.at[kind, ctx, piece],
+                kv_buf.at[slot, kind, piece], kv_out.at[kind, piece, ctx],
                 kv_send.at[slot, kind, piece], kv_recv.at[kind, ctx, piece], dest, head,
             ),
         )
@@ -818,14 +822,14 @@
     def beside(slot, piece):
         result = [
             remote(
-                query_buf.at[slot, piece, 1 - core], query_out.at[ctx, piece],
+                query_buf.at[slot, piece, 1 - core], query_out.at[piece, ctx],
                 q_send.at[slot, 1 - core, piece], q_recv.at[ctx, piece], ctx, partner,
             )
         ]
         for kind in range(2):
             result.append(
                 remote(
-                    kv_buf.at[slot, kind, piece], kv_out.at[kind, ctx, piece],
+                    kv_buf.at[slot, kind, piece], kv_out.at[kind, piece, ctx],
                     kv_send.at[slot, kind, piece], kv_recv.at[kind, ctx, piece], ctx, partner,
                 )
             )
@@ -836,7 +840,7 @@
         block = state_v[at(piece), :].astype(jnp.float32)
         normed = (block * row_scale(block) * gain).astype(jnp.bfloat16)
         for t in range(3):
-            result = jnp.dot(normed, w_v[t], preferred_element_type=jnp.float32).astype(
+            result = jnp.dot(normed, w_both[core, t], preferred_element_type=jnp.float32).astype(
                 jnp.bfloat16
             )
             for slot in range(slots):
@@ -859,9 +863,9 @@
 
             @pl.when(dest == ctx)
             def _():
-                query_out[ctx, piece] = query_buf[slot, piece, core]
+                query_out[piece, ctx] = query_buf[slot, piece, core]
                 for kind in range(2):
-                    kv_out[kind, ctx, piece] = kv_buf[slot, kind, piece]
+                    kv_out[kind, piece, ctx] = kv_buf[slot, kind, piece]
                 for copy in beside(slot, piece):
                     copy.start()
 
@@ -890,7 +894,7 @@
     def hand_over(piece, step):
         source = lax.rem(ctx + step, ctx_count)
         return remote(
-            kv_out.at[core, source, piece], kv_out.at[core, source, piece],
+            kv_out.at[core, piece, source], kv_out.at[core, piece, source],
             pass_send.at[step, piece], kv_recv.at[core, source, piece], ctx, partner,
         )
 
@@ -907,13 +911,13 @@
 
     def got_query(source, piece):
         remote(
-            query_out.at[source, piece], query_out.at[source, piece],
+            query_out.at[piece, source], query_out.at[piece, source],
             q_send.at[0, 0, piece], q_recv.at[source, piece], ctx, partner,
         ).wait_recv()
 
     def got_kv(kind, source, piece):
         remote(
-            kv_out.at[kind, source, piece], kv_out.at[kind, source, piece],
+            kv_out.at[kind, piece, source], kv_out.at[kind, piece, source],
             kv_send.at[0, 0, piece], kv_recv.at[kind, source, piece], ctx, partner,
         ).wait_recv()
 
@@ -935,21 +939,7 @@
     lax.fori_loop(0, groups, gather, 0)
     for copy in segs:
         copy.wait()
-    leaving = [
-        pltpu.make_async_copy(query_out.at[source], query_any.at[:, source], leave_sem.at[0, source])
-        for source in range(ctx_count)
-    ]
-    for kind in range(2):
-        leaving += [
-            pltpu.make_async_copy(
-                kv_out.at[kind, source], kv_any.at[kind, :, source],
-                leave_sem.at[1 + kind, source],
-            )
-            for source in range(ctx_count)
-        ]
-    for copy in leaving:
-        copy.start()
-    pair_copy = remote(w_any, w_pair, pair_send, pair_recv, ctx, partner)
+    pair_copy = remote(w_any, w_both.at[core], pair_send, pair_recv, ctx, partner)
     pair_copy.start()
 
     def cols_of(group_at, ctx_at):
@@ -973,12 +963,12 @@
 
     def out_copy(tile, order, other):
         return remote(
-            part_out.at[tile, other], joined.at[:, cols_of(group, ctx)],
+            part_out.at[other, tile], joined.at[:, cols_of(group, ctx)],
             out_send.at[tile, order], out_recv.at[group, ctx], tile, other * 2 + core,
         )
 
     def one_tile(tile, _):
-        query = query_out[tile].reshape(sub, HEAD_DIM)
+        query = query_out[:, tile].reshape(sub, HEAD_DIM)
         pos = (tile * rows + inside).astype(jnp.float32)
         start = jnp.where(
             pos >= second_bound, second_bound, jnp.where(pos >= first_bound, first_bound, 0.0)
@@ -986,7 +976,7 @@
 
         def step(diagonal, piece, carry):
             top, total, acc = carry
-            scores = dot32(kv_out[0, piece].reshape(rows, HEAD_DIM), query, NT)
+            scores = dot32(kv_out[0, :, piece].reshape(rows, HEAD_DIM), query, NT)
             allowed = key_row >= start - piece * rows
             if diagonal:
                 allowed = allowed & (key_row <= inside)
@@ -996,7 +986,7 @@
             scale = jnp.exp2(top - new_top)
             total = total * scale + jnp.sum(weights, axis=0, keepdims=True)
             acc = acc * scale + dot32(
-                kv_out[1, piece].reshape(rows, HEAD_DIM), weights.astype(jnp.bfloat16), TN
+                kv_out[1, :, piece].reshape(rows, HEAD_DIM), weights.astype(jnp.bfloat16), TN
             )
             return new_top, total, acc
 
@@ -1007,10 +997,11 @@
         )
         carry = lax.fori_loop(0, tile, functools.partial(step, False), carry)
         top, total, acc = step(True, tile, carry)
-        part_out[tile] = (acc / total).T.astype(jnp.bfloat16).reshape(groups, own, HEAD_DIM)
+        result = (acc / total).T.astype(jnp.bfloat16)
         log_row = top + jnp.log2(total)
         for index in range(groups):
-            log_out[index, :, own_at(tile)] = log_row[:, index * own : (index + 1) * own]
+            part_out[index, tile] = result[index * own : (index + 1) * own]
+            log_v[index, :, own_at(tile)] = log_row[:, index * own : (index + 1) * own]
         for order in range(groups):
             other = far_first(groups, group, order)
             if order == groups - 1:
@@ -1021,7 +1012,7 @@
 
                 @pl.when(tile == ctx)
                 def _():
-                    joined[:, cols_of(group, ctx)] = part_out[tile, group]
+                    joined[:, cols_of(group, ctx)] = part_out[group, tile]
 
             else:
                 out_copy(tile, order, other).start()
@@ -1033,13 +1024,6 @@
         return 0
 
     lax.fori_loop(0, ctx_count, one_tile, 0)
-    for source in range(ctx_count):
-        leaving.append(
-            pltpu.make_async_copy(
-                part_out.at[source], part_any.at[:, source], leave_sem.at[3, source]
-            )
-        )
-        leaving[-1].start()
     for copy in later_loads:
         copy.wait()
     sources = []
@@ -1117,8 +1101,6 @@
         return 0
 
     lax.fori_loop(0, model // tile, finish, 0)
-    leaving.append(pltpu.make_async_copy(readout_out, readout_any, leave_sem.at[4, 0]))
-    leaving[-1].start()
     copies = []
     for order in range(groups):
         other = far_first(groups, group, order)
@@ -1132,13 +1114,19 @@
             if order == groups - 1 and step == 0:
                 continue
             copy = remote(
-                sending.at[order, peer], grad_out.at[group, ctx], back_send.at[order, step],
+                sending.at[order, peer], grad_v.at[group, ctx], back_send.at[order, step],
                 back_recv.at[ctx, group], peer, other * 2 + core,
             )
             copy.start()
             copies.append(copy)
-    last = pltpu.make_async_copy(sending.at[groups - 1, ctx], grad_out.at[group, ctx], own_sem)
-    last.start()
+    grad_v[group, ctx] = sending[groups - 1, ctx]
+
+    def clear(index, _):
+        pair_acc[index] = jnp.zeros(pair_acc.shape[1:], jnp.float32)
+        query_acc[index] = jnp.zeros(query_acc.shape[1:], jnp.float32)
+        return 0
+
+    lax.fori_loop(0, groups, clear, 0)
 
     def sent(piece, _):
         for slot in range(slots):
@@ -1180,53 +1168,341 @@
     lax.fori_loop(0, ctx_count, parts_sent, 0)
     for other, peer in sources:
         remote(
-            sending.at[0, 0], grad_out.at[other, peer], back_send.at[0, 0],
+            sending.at[0, 0], grad_v.at[other, peer], back_send.at[0, 0],
             back_recv.at[peer, other], peer, other * 2 + core,
         ).wait_recv()
     for copy in copies:
         copy.wait_send()
-    last.wait()
-    for copy in leaving:
-        copy.wait()
     pair_copy.wait()
 
-
-def front(ctx_count, head_count, state, w_qkv, gain, segment_ids, w_out, probe):
+    halves = 2
+    span = ctx_count * own // halves
+    dests = [far_first(groups, group, order) for order in range(groups)]
+
+    def dest_of(order):
+        result = dests[0]
+        for index in range(1, groups):
+            result = jnp.where(order == index, dests[index], result)
+        return result
+
+    score_scale = HEAD_DIM ** (-0.5)
+    def half_of(ref, index, half):
+        count = ctx_count // halves
+        return ref[index, half * count : (half + 1) * count].reshape(span, HEAD_DIM)
+
+    def find_deltas(index, _):
+        for half in range(halves):
+            product = half_of(grad_v, index, half).astype(jnp.float32) * half_of(
+                part_out, index, half
+            ).astype(jnp.float32)
+            deltas[index, :, half * span : (half + 1) * span] = jnp.sum(
+                product.T, axis=0, keepdims=True
+            )
+        return 0
+
+    lax.fori_loop(0, groups, find_deltas, 0)
+    spot_lane = lax.broadcasted_iota(jnp.int32, (1, span), 1)
+
+    def pair(query_at, key_at):
+        for half in range(halves):
+            blocks = (half + 1) * ctx_count // halves
+            count = blocks * 2 * own
+            lanes = slice(half * span, (half + 1) * span)
+            key_block = kv_out[0, key_at, :blocks].reshape(count, HEAD_DIM)
+            value_block = kv_out[1, key_at, :blocks].reshape(count, HEAD_DIM)
+            query_block = half_of(query_out, query_at, half)
+            grad_block = half_of(grad_v, query_at, half)
+            spot = (half * (ctx_count // halves) + spot_lane // own) * rows + spot_lane % own
+            pos = spot + (query_at * 2 + core) * own
+            pos_f = pos.astype(jnp.float32)
+            start = jnp.where(
+                pos_f >= second_bound,
+                second_bound,
+                jnp.where(pos_f >= first_bound, first_bound, 0.0),
+            ).astype(jnp.int32)
+            line = lax.broadcasted_iota(jnp.int32, (count, span), 0)
+            key_pos = (line // (2 * own)) * rows + line % (2 * own)
+            offset = key_at * 2 * own
+            allowed = (key_pos >= start - offset) & (key_pos <= pos - offset)
+            scores = dot32(key_block, query_block, NT)
+            probabilities = jnp.where(
+                allowed, jnp.exp2(scores * factor - log_v[query_at, :, lanes]), 0.0
+            )
+            dprobs = dot32(value_block, grad_block, NT)
+            dscores = (probabilities * (dprobs - deltas[query_at, :, lanes])).astype(jnp.bfloat16)
+            pair_acc[key_at, :count, HEAD_DIM:] += jnp.dot(
+                probabilities.astype(jnp.bfloat16), grad_block, preferred_element_type=jnp.float32
+            )
+            pair_acc[key_at, :count, :HEAD_DIM] += jnp.dot(
+                dscores, query_block, preferred_element_type=jnp.float32
+            )
+            query_acc[query_at, :, lanes] += dot32(key_block, dscores, TN)
+
+    def core_copy(order):
+        return remote(
+            pair_buf.at[order], beside_in.at[order], b_send.at[order], b_recv.at[order], ctx, partner
+        )
+
+    def pair_rows(dest, source, kind):
+        first = pl.multiple_of((source * 2 + kind) * own, own)
+        keys = pair_acc[dest, pl.ds(first, own), :HEAD_DIM] * score_scale
+        values = pair_acc[dest, pl.ds(first, own), HEAD_DIM:]
+        return keys, values
+
+    def settle(order):
+        dest = dest_of(order)
+        for source in range(ctx_count):
+            keys, values = pair_rows(dest, source, 1 - core)
+            pair_buf[order, source, :, :HEAD_DIM] = keys.astype(jnp.bfloat16)
+            pair_buf[order, source, :, HEAD_DIM:] = values.astype(jnp.bfloat16)
+        for half in range(halves):
+            query_fin[order, half * span : (half + 1) * span, :] = (
+                query_acc[dest, :, half * span : (half + 1) * span].T * score_scale
+            ).astype(jnp.bfloat16)
+        core_copy(order).start()
+
+    def stripe(source):
+        slot = lax.rem(source, slots)
+        return pl.ds(pl.multiple_of(slot * HEAD_DIM, HEAD_DIM), HEAD_DIM)
+
+    def exchange(order, step):
+        peer = lax.rem(ctx + step, ctx_count)
+        return remote(
+            away_buf.at[order, step],
+            terms_in.at[dest_of(order), ctx // slots, :, :, stripe(ctx)],
+            a_send.at[order, step], a_recv.at[dest_of(order), ctx], peer, me,
+        )
+
+    def arrived(dest, step):
+        source = lax.rem(ctx + step, ctx_count)
+        remote(
+            away_buf.at[0, 0], terms_in.at[dest, source // slots, :, :, stripe(source)],
+            a_send.at[0, 0], a_recv.at[dest, source], source, me,
+        ).wait_recv()
+
+    def spread(order):
+        dest = dest_of(order)
+        core_copy(order).wait_recv()
+        for step in range(1, ctx_count + 1):
+            peer = lax.rem(ctx + step, ctx_count)
+            keys, values = pair_rows(dest, peer, core)
+            keys = (keys + beside_in[order, peer, :, :HEAD_DIM].astype(jnp.float32)).astype(
+                jnp.bfloat16
+            )
+            values = (values + beside_in[order, peer, :, HEAD_DIM:].astype(jnp.float32)).astype(
+                jnp.bfloat16
+            )
+            queries = query_fin[order, pl.ds(pl.multiple_of(peer * own, own), own), :]
+            if step < ctx_count:
+                away_buf[order, step, 0] = queries
+                away_buf[order, step, 1] = keys
+                away_buf[order, step, 2] = values
+                exchange(order, step).start()
+            else:
+                at = stripe(ctx)
+                terms_in[dest, ctx // slots, 0, :, at] = queries
+                terms_in[dest, ctx // slots, 1, :, at] = keys
+                terms_in[dest, ctx // slots, 2, :, at] = values
+
+    pieces = partial.shape[2]
+    strip = model // pieces
+
+    def chain(order, piece):
+        dest = dest_of(order)
+        up = dest > group
+        line = jnp.where(up, 0, 1)
+        peer = jnp.where(up, group + 1, group - 1)
+        return remote(
+            passing.at[order, piece], partial.at[line, dest, piece], z_send.at[order, piece],
+            z_recv.at[line, dest, piece], ctx, peer * 2 + core,
+        )
+
+    def came(line, dest, piece):
+        remote(
+            passing.at[0, piece], partial.at[line, dest, piece], z_send.at[0, piece],
+            z_recv.at[line, dest, piece], ctx, partner,
+        ).wait_recv()
+
+    def term(dest, piece):
+        cols = pl.ds(pl.multiple_of(piece * strip, strip), strip)
+        result = None
+        for half in range(2):
+            for kind in range(3):
+                part = dot32(terms_in[dest, half, kind], w_both[half, kind, cols, :], NT)
+                result = part if result is None else result + part
+        return result
+
+    inner = (group > 0) & (group < groups - 1)
+
+    def pass_on(order, _):
+        dest = dest_of(order)
+        for step in range(1, ctx_count):
+            arrived(dest, step)
+        line = jnp.where(dest > group, 0, 1)
+
+        def one_piece(piece, _):
+            sum_v[...] = term(dest, piece)
+
+            @pl.when(inner)
+            def _():
+                came(line, dest, piece)
+                sum_v[...] += partial[line, dest, piece].astype(jnp.float32)
+
+            passing[order, piece] = sum_v[...].astype(jnp.bfloat16)
+            chain(order, piece).start()
+            return 0
+
+        lax.fori_loop(0, pieces, one_piece, 0)
+        return 0
+
+    ends, number = [], 0
+    for order in range(groups):
+        number += 2 * (groups - order) - 1
+        ends.append(number - 1)
+    spreads = {order: end + 1 for order, end in enumerate(ends) if end + 1 < number}
+
+    def one_pair(index, _):
+        stage = 0
+        for end in ends[:-1]:
+            stage = stage + jnp.where(index > end, 1, 0)
+        first = 0
+        for order in range(1, groups):
+            first = jnp.where(stage == order, ends[order - 1] + 1, first)
+        inside = index - first
+        other = stage + (inside + 1) // 2
+        odd = lax.rem(inside, 2)
+        pair(
+            dest_of(jnp.where(odd == 1, stage, other)), dest_of(jnp.where(odd == 1, other, stage))
+        )
+        for order, end in enumerate(ends[:-1]):
+
+            @pl.when(index == end)
+            def _():
+                settle(order)
+
+        for order, at in spreads.items():
+
+            @pl.when(index == at)
+            def _():
+                spread(order)
+
+        return 0
+
+    first = min(ends[min(1, groups - 1)] + 2, number)
+    lax.fori_loop(0, first, one_pair, 0)
+    early = 1 if first < number else 0
+    if early:
+
+        @pl.when(jnp.logical_not(inner))
+        def _():
+            pass_on(0, 0)
+
+        lax.fori_loop(first, number, one_pair, 0)
+    settle(groups - 1)
+    for order in range(groups):
+        if order not in spreads:
+            spread(order)
+    lax.fori_loop(jnp.where(inner, 0, early), groups - 1, pass_on, 0)
+    for step in range(1, ctx_count):
+        arrived(group, step)
+
+    state = state_own[...].astype(jnp.float32)
+    inverse = row_scale(state)
+
+    def last_piece(piece, slope):
+        cols = pl.ds(pl.multiple_of(piece * strip, strip), strip)
+        sum_v[...] = term(group, piece)
+
+        @pl.when(group > 0)
+        def _():
+            came(0, group, piece)
+            sum_v[...] += partial[0, group, piece].astype(jnp.float32)
+
+        @pl.when(group < groups - 1)
+        def _():
+            came(1, group, piece)
+            sum_v[...] += partial[1, group, piece].astype(jnp.float32)
+
+        gained = sum_v[...] * gain_ref[cols].astype(jnp.float32).reshape(1, strip)
+        new_out[:, cols] = gained
+        return slope + jnp.sum(
+            gained * state_own[:, cols].astype(jnp.float32), axis=1, keepdims=True
+        )
+
+    slope = lax.fori_loop(0, pieces, last_piece, jnp.zeros((own, 1), jnp.float32))
+    bend = inverse**3 * (slope / model)
+
+    def update(piece, _):
+        cols = pl.ds(pl.multiple_of(piece * strip, strip), strip)
+        here = state_own[:, cols].astype(jnp.float32)
+        gradient = readout_out[:, cols] + inverse * new_out[:, cols] - here * bend
+        new_out[:, cols] = (
+            here - STEP_SIZE * gradient + NOISE_SCALE * noise_own[:, cols].astype(jnp.float32)
+        )
+        return 0
+
+    lax.fori_loop(0, pieces, update, 0)
+
+    def all_sent(order, _):
+        core_copy(order).wait_send()
+        for step in range(1, ctx_count):
+            exchange(order, step).wait_send()
+
+        @pl.when(order < groups - 1)
+        def _():
+            for piece in range(pieces):
+                chain(order, piece).wait_send()
+
+        return 0
+
+    lax.fori_loop(0, groups, all_sent, 0)
+
+
+def heads_body(state, norm_gain, w_qkv, w_out, probe, noise, segment_ids):
+    ctx_count, head_count = lax.axis_size("ctx"), lax.axis_size("head")
     rows, model = state.shape
     width = w_qkv.shape[2]
     own, groups, slots = rows // head_count, head_count // 2, width // HEAD_DIM
     seg = segment_ids.reshape(-1, 128)
     half, full, dma = jnp.bfloat16, jnp.float32, pltpu.SemaphoreType.DMA
-    shape = jax.ShapeDtypeStruct
+    pieces, lanes = 4, ctx_count * own
+    tile, vmem = model // pieces, pltpu.VMEM
+    heads = (groups, ctx_count, own, HEAD_DIM)
     return pl.pallas_call(
-        functools.partial(front_kernel, ctx_count, head_count),
-        out_shape=(
-            shape((groups, ctx_count, own, HEAD_DIM), half),
-            shape((2, groups, ctx_count, 2 * own, HEAD_DIM), half),
-            shape((ctx_count,) + seg.shape, seg.dtype),
-            shape((groups, ctx_count, own, HEAD_DIM), half),
-            shape((groups, 1, ctx_count * own), full),
-            shape((groups, ctx_count, own, HEAD_DIM), half),
-            shape((own, model), full),
-            shape(w_qkv.shape, half),
-        ),
-        in_specs=[ANY, ANY, VMEM, VMEM, ANY, ANY],
-        out_specs=(ANY, ANY, VMEM, ANY, VMEM, ANY, ANY, ANY),
+        functools.partial(step_kernel, ctx_count, head_count),
+        out_shape=jax.ShapeDtypeStruct((own, model), full),
+        in_specs=[ANY, ANY, VMEM, VMEM, ANY, ANY, ANY],
+        out_specs=VMEM,
         scratch_shapes=[
-            pltpu.VMEM((rows, model), half),
-            pltpu.VMEM(w_qkv.shape, half),
-            pltpu.VMEM((slots, groups, 2, own, HEAD_DIM), half),
-            pltpu.VMEM((slots, 2, groups, 2 * own, HEAD_DIM), half),
-            pltpu.VMEM((model, model), half),
-            pltpu.VMEM((own, model), half),
-            pltpu.VMEM((own, model), half),
-            pltpu.VMEM((groups, ctx_count, own, HEAD_DIM), half),
-            pltpu.VMEM((own, model), half),
-            pltpu.VMEM((own, model), half),
-            pltpu.VMEM((ctx_count, groups, own, HEAD_DIM), half),
-            pltpu.VMEM((2, ctx_count, groups, 2 * own, HEAD_DIM), half),
-            pltpu.VMEM((ctx_count, groups, own, HEAD_DIM), half),
-            pltpu.VMEM((own, model), full),
+            vmem((rows, model), half),
+            vmem((slots, groups, 2, own, HEAD_DIM), half),
+            vmem((slots, 2, groups, 2 * own, HEAD_DIM), half),
+            vmem((model, model), half),
+            vmem((own, model), half),
+            vmem((own, model), half),
+            vmem(heads, half),
+            vmem((own, model), half),
+            vmem((own, model), half),
+            vmem((own, model), half),
+            vmem(heads, half),
+            vmem((2, groups, ctx_count, 2 * own, HEAD_DIM), half),
+            vmem(heads, half),
+            vmem((own, model), full),
+            vmem((ctx_count,) + seg.shape, seg.dtype),
+            vmem((groups, 1, lanes), full),
+            vmem(heads, half),
+            vmem((2,) + w_qkv.shape, half),
+            vmem((groups, 2 * lanes, 2 * HEAD_DIM), full),
+            vmem((groups, HEAD_DIM, lanes), full),
+            vmem((groups, 1, lanes), full),
+            vmem((groups, lanes, HEAD_DIM), half),
+            vmem((groups, ctx_count, own, 2 * HEAD_DIM), half),
+            vmem((groups, ctx_count, own, 2 * HEAD_DIM), half),
+            vmem((groups, ctx_count, 3, own, HEAD_DIM), half),
+            vmem((groups, 2, 3, own, width), half),
+            vmem((2, groups, pieces, own, tile), half),
+            vmem((groups, pieces, own, tile), half),
+            vmem((own, tile), full),
             dma((groups,)),
             dma((3,)),
             dma((slots, 2, groups)),
@@ -1249,418 +1525,20 @@
             dma((groups, ctx_count)),
             dma((groups, ctx_count)),
             dma((ctx_count, groups)),
-            dma,
-            dma((2,)),
+            dma((3,)),
             dma,
             dma,
-            dma((5, ctx_count)),
-        ],
-        compiler_params=pltpu.CompilerParams(
-            collective_id=0, has_side_effects=True, vmem_limit_bytes=62 * 2**20
-        ),
-    )(state, w_qkv, gain, seg, w_out, probe)
-
-
-def back_kernel(
-    ctx_count, head_count, query_any, kv_any, grad_any, part_any, segs_ref, log_ref, w_any, w_pair,
-    state_any, noise_any, readout_any, gain_ref, new_out, query_v, kv_v, grad_v, part_v, pair_acc,
-    query_acc, deltas, query_fin, pair_buf, w_both, beside, away, terms_in, partial, sending, total,
-    state_own, noise_own, readout_own, in_sem, b_send, b_recv, a_send, a_recv, z_send, z_recv,
-    own_sem,
-):
-    ctx, me, group, core = place()
-    groups = head_count // 2
-    own, model = new_out.shape
-    slots, halves = ctx_count // 2, 2
-    rows = groups * 2 * own
-    sub = ctx_count * own // halves
-    partner = group * 2 + 1 - core
-    my_rows = pl.ds(pl.multiple_of(me * own, own), own)
-    inputs = [
-        pltpu.make_async_copy(source, target, in_sem.at[index])
-        for index, (source, target) in enumerate(
-            ((grad_any, grad_v), (part_any, part_v), (query_any, query_v), (kv_any, kv_v))
-        )
-    ]
-    loads = [
-        pltpu.make_async_copy(w_any, w_both.at[core], own_sem.at[0]),
-        pltpu.make_async_copy(w_pair, w_both.at[1 - core], own_sem.at[1]),
-        pltpu.make_async_copy(state_any.at[my_rows], state_own, own_sem.at[2]),
-        pltpu.make_async_copy(noise_any, noise_own, own_sem.at[3]),
-        pltpu.make_async_copy(readout_any, readout_own, own_sem.at[4]),
-    ]
-    for copy in inputs:
-        copy.start()
-    peers = [(ctx, partner)]
-    peers += [(lax.rem(ctx + step, ctx_count), me) for step in range(1, ctx_count)]
-    peers += [(ctx, lax.rem(group + far, groups) * 2 + core) for far in range(1, groups)]
-    announce(peers)
-    dests = [far_first(groups, group, order) for order in range(groups)]
-
-    def dest_of(order):
-        result = dests[0]
-        for index in range(1, groups):
-            result = jnp.where(order == index, dests[index], result)
-        return result
-
-    score_scale = HEAD_DIM ** (-0.5)
-    factor = score_scale * LOG2E
-    seg_all = segs_ref[...]
-
-    def below(value):
-        count = jnp.where(seg_all < value, 1.0, 0.0)
-        for axis in (0, 1, 2):
-            count = jnp.sum(count, axis=axis, keepdims=True)
-        return count[0]
-
-    first_bound, second_bound = below(1), below(2)
-
-    def clear(index, _):
-        pair_acc[index] = jnp.zeros(pair_acc.shape[1:], jnp.float32)
-        query_acc[index] = jnp.zeros(query_acc.shape[1:], jnp.float32)
-        return 0
-
-    lax.fori_loop(0, groups, clear, 0)
-    for copy in inputs:
-        copy.wait()
-    for copy in loads:
-        copy.start()
-
-    def half_of(ref, index, half):
-        count = ctx_count // halves
-        return ref[index, half * count : (half + 1) * count].reshape(sub, HEAD_DIM)
-
-    def find_deltas(index, _):
-        for half in range(halves):
-            product = half_of(grad_v, index, half).astype(jnp.float32) * half_of(
-                part_v, index, half
-            ).astype(jnp.float32)
-            deltas[index, :, half * sub : (half + 1) * sub] = jnp.sum(
-                product.T, axis=0, keepdims=True
-            )
-        return 0
-
-    lax.fori_loop(0, groups, find_deltas, 0)
-    await_all(peers)
-    lane = lax.broadcasted_iota(jnp.int32, (1, sub), 1)
-
-    def pair(query_at, key_at):
-        for half in range(halves):
-            blocks = (half + 1) * ctx_count // halves
-            count = blocks * 2 * own
-            lanes = slice(half * sub, (half + 1) * sub)
-            key_block = kv_v[0, key_at, :blocks].reshape(count, HEAD_DIM)
-            value_block = kv_v[1, key_at, :blocks].reshape(count, HEAD_DIM)
-            query_block = half_of(query_v, query_at, half)
-            grad_block = half_of(grad_v, query_at, half)
-            spot = (half * (ctx_count // halves) + lane // own) * rows + lane % own
-            pos = spot + (query_at * 2 + core) * own
-            pos_f = pos.astype(jnp.float32)
-            start = jnp.where(
-                pos_f >= second_bound,
-                second_bound,
-                jnp.where(pos_f >= first_bound, first_bound, 0.0),
-            ).astype(jnp.int32)
-            line = lax.broadcasted_iota(jnp.int32, (count, sub), 0)
-            key_pos = (line // (2 * own)) * rows + line % (2 * own)
-            offset = key_at * 2 * own
-            allowed = (key_pos >= start - offset) & (key_pos <= pos - offset)
-            scores = dot32(key_block, query_block, NT)
-            probabilities = jnp.where(
-                allowed, jnp.exp2(scores * factor - log_ref[query_at, :, lanes]), 0.0
-            )
-            dprobs = dot32(value_block, grad_block, NT)
-            dscores = (probabilities * (dprobs - deltas[query_at, :, lanes])).astype(jnp.bfloat16)
-            pair_acc[key_at, :count, HEAD_DIM:] += jnp.dot(
-                probabilities.astype(jnp.bfloat16), grad_block, preferred_element_type=jnp.float32
-            )
-            pair_acc[key_at, :count, :HEAD_DIM] += jnp.dot(
-                dscores, query_block, preferred_element_type=jnp.float32
-            )
-            query_acc[query_at, :, lanes] += dot32(key_block, dscores, TN)
-
-    def beside_copy(order):
-        return remote(
-            pair_buf.at[order], beside.at[order], b_send.at[order], b_recv.at[order], ctx, partner
-        )
-
-    def pair_rows(dest, source, kind):
-        first = pl.multiple_of((source * 2 + kind) * own, own)
-        keys = pair_acc[dest, pl.ds(first, own), :HEAD_DIM] * score_scale
-        values = pair_acc[dest, pl.ds(first, own), HEAD_DIM:]
-        return keys, values
-
-    def settle(order):
-        dest = dest_of(order)
-        for source in range(ctx_count):
-            keys, values = pair_rows(dest, source, 1 - core)
-            pair_buf[order, source, :, :HEAD_DIM] = keys.astype(jnp.bfloat16)
-            pair_buf[order, source, :, HEAD_DIM:] = values.astype(jnp.bfloat16)
-        for half in range(halves):
-            query_fin[order, half * sub : (half + 1) * sub, :] = (
-                query_acc[dest, :, half * sub : (half + 1) * sub].T * score_scale
-            ).astype(jnp.bfloat16)
-        beside_copy(order).start()
-
-    def stripe(source):
-        slot = lax.rem(source, slots)
-        return pl.ds(pl.multiple_of(slot * HEAD_DIM, HEAD_DIM), HEAD_DIM)
-
-    def exchange(order, step):
-        peer = lax.rem(ctx + step, ctx_count)
-        return remote(
-            away.at[order, step],
-            terms_in.at[dest_of(order), ctx // slots, :, :, stripe(ctx)],
-            a_send.at[order, step], a_recv.at[dest_of(order), ctx], peer, me,
-        )
-
-    def arrived(dest, step):
-        source = lax.rem(ctx + step, ctx_count)
-        remote(
-            away.at[0, 0], terms_in.at[dest, source // slots, :, :, stripe(source)],
-            a_send.at[0, 0], a_recv.at[dest, source], source, me,
-        ).wait_recv()
-
-    def spread(order):
-        dest = dest_of(order)
-        beside_copy(order).wait_recv()
-        for step in range(1, ctx_count + 1):
-            peer = lax.rem(ctx + step, ctx_count)
-            keys, values = pair_rows(dest, peer, core)
-            keys = (keys + beside[order, peer, :, :HEAD_DIM].astype(jnp.float32)).astype(
-                jnp.bfloat16
-            )
-            values = (values + beside[order, peer, :, HEAD_DIM:].astype(jnp.float32)).astype(
-                jnp.bfloat16
-            )
-            queries = query_fin[order, pl.ds(pl.multiple_of(peer * own, own), own), :]
-            if step < ctx_count:
-                away[order, step, 0] = queries
-                away[order, step, 1] = keys
-                away[order, step, 2] = values
-                exchange(order, step).start()
-            else:
-                at = stripe(ctx)
-                terms_in[dest, ctx // slots, 0, :, at] = queries
-                terms_in[dest, ctx // slots, 1, :, at] = keys
-                terms_in[dest, ctx // slots, 2, :, at] = values
-
-    pieces = partial.shape[2]
-    tile = model // pieces
-
-    def chain(order, piece):
-        dest = dest_of(order)
-        up = dest > group
-        line = jnp.where(up, 0, 1)
-        peer = jnp.where(up, group + 1, group - 1)
-        return remote(
-            sending.at[order, piece], partial.at[line, dest, piece], z_send.at[order, piece],
-            z_recv.at[line, dest, piece], ctx, peer * 2 + core,
-        )
-
-    def came(line, dest, piece):
-        remote(
-            sending.at[0, piece], partial.at[line, dest, piece], z_send.at[0, piece],
-            z_recv.at[line, dest, piece], ctx, partner,
-        ).wait_recv()
-
-    def term(dest, piece):
-        cols = pl.ds(pl.multiple_of(piece * tile, tile), tile)
-        result = None
-        for half in range(2):
-            for kind in range(3):
-                part = dot32(terms_in[dest, half, kind], w_both[half, kind, cols, :], NT)
-                result = part if result is None else result + part
-        return result
-
-    inner = (group > 0) & (group < groups - 1)
-
-    def pass_on(order, _):
-        dest = dest_of(order)
-        for step in range(1, ctx_count):
-            arrived(dest, step)
-        line = jnp.where(dest > group, 0, 1)
-
-        def one_piece(piece, _):
-            total[...] = term(dest, piece)
-
-            @pl.when(inner)
-            def _():
-                came(line, dest, piece)
-                total[...] += partial[line, dest, piece].astype(jnp.float32)
-
-            sending[order, piece] = total[...].astype(jnp.bfloat16)
-            chain(order, piece).start()
-            return 0
-
-        lax.fori_loop(0, pieces, one_piece, 0)
-        return 0
-
-    ends, number = [], 0
-    for order in range(groups):
-        number += 2 * (groups - order) - 1
-        ends.append(number - 1)
-    spreads = {order: end + 1 for order, end in enumerate(ends) if end + 1 < number}
-
-    def one_pair(index, _):
-        stage = 0
-        for end in ends[:-1]:
-            stage = stage + jnp.where(index > end, 1, 0)
-        first = 0
-        for order in range(1, groups):
-            first = jnp.where(stage == order, ends[order - 1] + 1, first)
-        inside = index - first
-        other = stage + (inside + 1) // 2
-        odd = lax.rem(inside, 2)
-        pair(
-            dest_of(jnp.where(odd == 1, stage, other)), dest_of(jnp.where(odd == 1, other, stage))
-        )
-        for order, end in enumerate(ends[:-1]):
-
-            @pl.when(index == end)
-            def _():
-                settle(order)
-
-        for order, at in spreads.items():
-
-            @pl.when(index == at)
-            def _():
-                spread(order)
-
-        return 0
-
-    first = min(ends[min(1, groups - 1)] + 2, number)
-    lax.fori_loop(0, first, one_pair, 0)
-    for copy in loads:
-        copy.wait()
-    early = 1 if first < number else 0
-    if early:
-
-        @pl.when(jnp.logical_not(inner))
-        def _():
-            pass_on(0, 0)
-
-        lax.fori_loop(first, number, one_pair, 0)
-    settle(groups - 1)
-    for order in range(groups):
-        if order not in spreads:
-            spread(order)
-    lax.fori_loop(jnp.where(inner, 0, early), groups - 1, pass_on, 0)
-    for step in range(1, ctx_count):
-        arrived(group, step)
-
-    state = state_own[...].astype(jnp.float32)
-    inverse = row_scale(state)
-
-    def last_piece(piece, slope):
-        cols = pl.ds(pl.multiple_of(piece * tile, tile), tile)
-        total[...] = term(group, piece)
-
-        @pl.when(group > 0)
-        def _():
-            came(0, group, piece)
-            total[...] += partial[0, group, piece].astype(jnp.float32)
-
-        @pl.when(group < groups - 1)
-        def _():
-            came(1, group, piece)
-            total[...] += partial[1, group, piece].astype(jnp.float32)
-
-        gained = total[...] * gain_ref[cols].astype(jnp.float32).reshape(1, tile)
-        new_out[:, cols] = gained
-        return slope + jnp.sum(
-            gained * state_own[:, cols].astype(jnp.float32), axis=1, keepdims=True
-        )
-
-    slope = lax.fori_loop(0, pieces, last_piece, jnp.zeros((own, 1), jnp.float32))
-    bend = inverse**3 * (slope / model)
-
-    def update(piece, _):
-        cols = pl.ds(pl.multiple_of(piece * tile, tile), tile)
-        here = state_own[:, cols].astype(jnp.float32)
-        gradient = readout_own[:, cols] + inverse * new_out[:, cols] - here * bend
-        new_out[:, cols] = (
-            here - STEP_SIZE * gradient + NOISE_SCALE * noise_own[:, cols].astype(jnp.float32)
-        )
-        return 0
-
-    lax.fori_loop(0, pieces, update, 0)
-
-    def sent(order, _):
-        beside_copy(order).wait_send()
-        for step in range(1, ctx_count):
-            exchange(order, step).wait_send()
-
-        @pl.when(order < groups - 1)
-        def _():
-            for piece in range(pieces):
-                chain(order, piece).wait_send()
-
-        return 0
-
-    lax.fori_loop(0, groups, sent, 0)
-
-
-def back(
-    ctx_count, head_count, queries, kv, grads, parts, segs, logs, w_qkv, w_pair, state, noise,
-    readout, gain,
-):
-    own, model = readout.shape
-    width = w_qkv.shape[2]
-    groups, pieces = head_count // 2, 4
-    half, full, dma = jnp.bfloat16, jnp.float32, pltpu.SemaphoreType.DMA
-    tile, lanes = model // pieces, ctx_count * own
-    return pl.pallas_call(
-        functools.partial(back_kernel, ctx_count, head_count),
-        out_shape=jax.ShapeDtypeStruct((own, model), full),
-        in_specs=[ANY] * 4 + [VMEM] * 2 + [ANY] * 5 + [VMEM],
-        out_specs=VMEM,
-        scratch_shapes=[
-            pltpu.VMEM(queries.shape, half),
-            pltpu.VMEM(kv.shape, half),
-            pltpu.VMEM(queries.shape, half),
-            pltpu.VMEM(queries.shape, half),
-            pltpu.VMEM((groups, 2 * lanes, 2 * HEAD_DIM), full),
-            pltpu.VMEM((groups, HEAD_DIM, lanes), full),
-            pltpu.VMEM((groups, 1, lanes), full),
-            pltpu.VMEM((groups, lanes, HEAD_DIM), half),
-            pltpu.VMEM((groups, ctx_count, own, 2 * HEAD_DIM), half),
-            pltpu.VMEM((2,) + w_qkv.shape, half),
-            pltpu.VMEM((groups, ctx_count, own, 2 * HEAD_DIM), half),
-            pltpu.VMEM((groups, ctx_count, 3, own, HEAD_DIM), half),
-            pltpu.VMEM((groups, 2, 3, own, width), half),
-            pltpu.VMEM((2, groups, pieces, own, tile), half),
-            pltpu.VMEM((groups, pieces, own, tile), half),
-            pltpu.VMEM((own, tile), full),
-            pltpu.VMEM((own, model), half),
-            pltpu.VMEM((own, model), half),
-            pltpu.VMEM((own, model), full),
-            dma((4,)),
             dma((groups,)),
             dma((groups,)),
             dma((groups, ctx_count)),
             dma((groups, ctx_count)),
             dma((groups, pieces)),
             dma((2, groups, pieces)),
-            dma((5,)),
         ],
         compiler_params=pltpu.CompilerParams(
-            collective_id=2, has_side_effects=True, vmem_limit_bytes=62 * 2**20
+            collective_id=0, has_side_effects=True, vmem_limit_bytes=63 * 2**20
         ),
-    )(
-        queries, kv, grads, parts, segs, logs, w_qkv, w_pair, state, noise, readout, gain,
-    )
-
-
-def heads_body(state, norm_gain, w_qkv, w_out, probe, noise, segment_ids):
-    head_count, ctx_count = lax.axis_size("head"), lax.axis_size("ctx")
-    queries, kv, segs, parts, logs, grads, readout, w_pair = front(
-        ctx_count, head_count, state, w_qkv, norm_gain, segment_ids, w_out, probe
-    )
-    return back(
-        ctx_count, head_count, queries, kv, grads, parts, segs, logs, w_qkv, w_pair, state, noise,
-        readout, norm_gain,
-    )
+    )(state, w_qkv, norm_gain, seg, w_out, probe, noise)
 
 
 def solution(mesh):

time: 141 us -> 136 us (0.965)
  Pallas kernels: 138 us -> 134 us
    pallas_call x2 -> x1, Pallas kernels: 138 us -> 134 us  [heads_body(): pl.pallas_call(functools.partial(step_kernel, ctx_count, head_count), out...]
where the time goes in v2:
time: 136 us
  Pallas kernels  134 us (99%)
  local copies, waits for them, and re-layouts  2.3 us (2%)
    pallas_call x1, Pallas kernels, heads_body(): pl.pallas_call(functools.partial(step_kernel, ctx_count, head_count), out...  134 us

profile of v2, /device:TPU:0, one launch (start us, length us, event | category | flops | bytes accessed | tf_op | source)
XLA Modules:
  0.0 135.8 jit_solution(10159967122485090675)
XLA Ops:
  0.0 133.5 %shard_map.73 = f32[128,2048]{1,0:T(8,128)} custom-call(bf16[1024,2048]{1,0:T(8,128)(2,1)} %state_any.1, bf16[3,2048,256]{2,1,0:T(8,128)(2,1)} %w_any.1, bf16[2048]{0:T(1024)(128)(2,1)} %gain_ref.1, s32[8,128]{1,0:T(8,128)} %bitcast.1, bf16[256,2048]{1,0:T(8,128)(2,1)} %w_out_any.1, bf16[1024,2048]{1,0:T(8,128)(2,1)} %probe_any.1, bf16[128,2048]{1,0:T(8,128)(2,1)} %noise_any.1), custom_call_target="tpu_custom_call" | custom-call | tf_op jit(solution)/shard_map/pallas_call | solution.py:1471
  133.5 2.3 %copy.9 = f32[128,2048]{1,0:T(8,128)} copy(f32[128,2048]{1,0:T(8,128)} %shard_map.73) | data formatting | bytes 2097152

commit v3 on v2

--- a/solution.py
+++ b/solution.py
@@ -649,6 +649,18 @@
     return result
 
 
+def by_arrival(groups, group, step):
+    result = 0
+    for index in range(groups):
+        last = sorted(range(groups), key=lambda other: (-abs(other - index), -other))[0]
+        order = sorted(
+            (other for other in range(groups) if other != last),
+            key=lambda other: (other in (0, groups - 1), abs(other - index)),
+        )
+        result = jnp.where(group == index, (order + [last])[step], result)
+    return result
+
+
 def step_kernel(
     ctx_count, head_count, state_any, w_any, gain_ref, seg_ref, w_out_any, probe_any, noise_any,
     new_out, state_v, query_buf, kv_buf, w_ref, joined, half, sending, state_own, probe_own,
@@ -1166,15 +1178,6 @@
         return 0
 
     lax.fori_loop(0, ctx_count, parts_sent, 0)
-    for other, peer in sources:
-        remote(
-            sending.at[0, 0], grad_v.at[other, peer], back_send.at[0, 0],
-            back_recv.at[peer, other], peer, other * 2 + core,
-        ).wait_recv()
-    for copy in copies:
-        copy.wait_send()
-    pair_copy.wait()
-
     halves = 2
     span = ctx_count * own // halves
     dests = [far_first(groups, group, order) for order in range(groups)]
@@ -1190,7 +1193,7 @@
         count = ctx_count // halves
         return ref[index, half * count : (half + 1) * count].reshape(span, HEAD_DIM)
 
-    def find_deltas(index, _):
+    def find_deltas(index):
         for half in range(halves):
             product = half_of(grad_v, index, half).astype(jnp.float32) * half_of(
                 part_out, index, half
@@ -1198,10 +1201,21 @@
             deltas[index, :, half * span : (half + 1) * span] = jnp.sum(
                 product.T, axis=0, keepdims=True
             )
-        return 0
-
-    lax.fori_loop(0, groups, find_deltas, 0)
+
+    def gradients_arrived(other):
+        for peer in range(ctx_count):
+
+            @pl.when(jnp.logical_or(other != group, ctx != peer))
+            def _():
+                remote(
+                    sending.at[0, 0], grad_v.at[other, peer], back_send.at[0, 0],
+                    back_recv.at[peer, other], ctx, partner,
+                ).wait_recv()
+
+        find_deltas(other)
+
     spot_lane = lax.broadcasted_iota(jnp.int32, (1, span), 1)
+    key_line = lax.broadcasted_iota(jnp.int32, (2 * own, own), 0)
 
     def pair(query_at, key_at):
         for half in range(halves):
@@ -1212,22 +1226,33 @@
             value_block = kv_out[1, key_at, :blocks].reshape(count, HEAD_DIM)
             query_block = half_of(query_out, query_at, half)
             grad_block = half_of(grad_v, query_at, half)
-            spot = (half * (ctx_count // halves) + spot_lane // own) * rows + spot_lane % own
-            pos = spot + (query_at * 2 + core) * own
+            first_ctx = half * (ctx_count // halves)
+            pos = (first_ctx + spot_lane // own) * rows + spot_lane % own
+            pos = pos + (query_at * 2 + core) * own
             pos_f = pos.astype(jnp.float32)
             start = jnp.where(
                 pos_f >= second_bound,
                 second_bound,
                 jnp.where(pos_f >= first_bound, first_bound, 0.0),
             ).astype(jnp.int32)
-            line = lax.broadcasted_iota(jnp.int32, (count, span), 0)
-            key_pos = (line // (2 * own)) * rows + line % (2 * own)
-            offset = key_at * 2 * own
-            allowed = (key_pos >= start - offset) & (key_pos <= pos - offset)
             scores = dot32(key_block, query_block, NT)
-            probabilities = jnp.where(
-                allowed, jnp.exp2(scores * factor - log_v[query_at, :, lanes]), 0.0
-            )
+            raw = jnp.exp2(scores * factor - log_v[query_at, :, lanes])
+            strips = []
+            for source in range(blocks):
+                offset = source * rows + key_at * 2 * own
+                row_cut = slice(source * 2 * own, (source + 1) * 2 * own)
+                cells = []
+                for index in range(ctx_count // halves):
+                    lane_cut = slice(index * own, (index + 1) * own)
+                    if source > first_ctx + index:
+                        cells.append(jnp.zeros((2 * own, own), jnp.float32))
+                        continue
+                    allowed = key_line >= start[:, lane_cut] - offset
+                    if source == first_ctx + index:
+                        allowed = allowed & (key_line <= pos[:, lane_cut] - offset)
+                    cells.append(jnp.where(allowed, raw[row_cut, lane_cut], 0.0))
+                strips.append(jnp.concatenate(cells, axis=1))
+            probabilities = jnp.concatenate(strips, axis=0)
             dprobs = dot32(value_block, grad_block, NT)
             dscores = (probabilities * (dprobs - deltas[query_at, :, lanes])).astype(jnp.bfloat16)
             pair_acc[key_at, :count, HEAD_DIM:] += jnp.dot(
@@ -1374,7 +1399,7 @@
         pair(
             dest_of(jnp.where(odd == 1, stage, other)), dest_of(jnp.where(odd == 1, other, stage))
         )
-        for order, end in enumerate(ends[:-1]):
+        for order, end in list(enumerate(ends))[1:-1]:
 
             @pl.when(index == end)
             def _():
@@ -1388,8 +1413,26 @@
 
         return 0
 
+    def farthest_pair(index, _):
+        arriving = index < groups
+        other = 0
+        for step in range(groups):
+            visit = by_arrival(groups, group, step)
+            other = jnp.where(index == step, visit, other)
+            other = jnp.where(index == groups + step, visit, other)
+
+        @pl.when(arriving)
+        def _():
+            gradients_arrived(other)
+
+        pair(jnp.where(arriving, other, dests[0]), jnp.where(arriving, dests[0], other))
+        return 0
+
     first = min(ends[min(1, groups - 1)] + 2, number)
-    lax.fori_loop(0, first, one_pair, 0)
+    lax.fori_loop(0, ends[0] + 1, farthest_pair, 0)
+    settle(0)
+    lax.fori_loop(ends[0] + 1, first, one_pair, 0)
+    pair_copy.wait()
     early = 1 if first < number else 0
     if early:
 
@@ -1455,6 +1498,8 @@
 
         return 0
 
+    for copy in copies:
+        copy.wait_send()
     lax.fori_loop(0, groups, all_sent, 0)
 
 

time: 136 us -> 131 us (0.963)
  Pallas kernels: 134 us -> 128 us
    pallas_call x1, Pallas kernels: 134 us -> 128 us  [heads_body(): pl.pallas_call(functools.partial(step_kernel, ctx_count, head_count), out...]
where the time goes in v3:
time: 131 us
  Pallas kernels  128 us (98%)
  local copies, waits for them, and re-layouts  2.3 us (2%)
    pallas_call x1, Pallas kernels, heads_body(): pl.pallas_call(functools.partial(step_kernel, ctx_count, head_count), out...  128 us

profile of v3, /device:TPU:0, one launch (start us, length us, event | category | flops | bytes accessed | tf_op | source)
XLA Modules:
  0.0 130.8 jit_solution(12571010471238811635)
XLA Ops:
  0.0 128.5 %shard_map.73 = f32[128,2048]{1,0:T(8,128)} custom-call(bf16[1024,2048]{1,0:T(8,128)(2,1)} %state_any.1, bf16[3,2048,256]{2,1,0:T(8,128)(2,1)} %w_any.1, bf16[2048]{0:T(1024)(128)(2,1)} %gain_ref.1, s32[8,128]{1,0:T(8,128)} %bitcast.1, bf16[256,2048]{1,0:T(8,128)(2,1)} %w_out_any.1, bf16[1024,2048]{1,0:T(8,128)(2,1)} %probe_any.1, bf16[128,2048]{1,0:T(8,128)(2,1)} %noise_any.1), custom_call_target="tpu_custom_call" | custom-call | tf_op jit(solution)/shard_map/pallas_call | solution.py:1516
  128.5 2.3 %copy.9 = f32[128,2048]{1,0:T(8,128)} copy(f32[128,2048]{1,0:T(8,128)} %shard_map.73) | data formatting | bytes 2097152

commit v4 on v3

--- a/solution.py
+++ b/solution.py
@@ -1043,7 +1043,7 @@
         for step in range(ctx_count):
             if far or step:
                 sources.append((lax.rem(group + far, groups), lax.rem(ctx + step, ctx_count)))
-    tile = min(256, model)
+    tile = min(512, model)
     wide = ctx_count * HEAD_DIM
     zero = jnp.zeros((own, 1), jnp.float32)
     for axis in range(2):
@@ -1428,7 +1428,7 @@
         pair(jnp.where(arriving, other, dests[0]), jnp.where(arriving, dests[0], other))
         return 0
 
-    first = min(ends[min(1, groups - 1)] + 2, number)
+    first = min(ends[min(1, groups - 1)] + 1, number)
     lax.fori_loop(0, ends[0] + 1, farthest_pair, 0)
     settle(0)
     lax.fori_loop(ends[0] + 1, first, one_pair, 0)
@@ -1581,7 +1581,7 @@
             dma((2, groups, pieces)),
         ],
         compiler_params=pltpu.CompilerParams(
-            collective_id=0, has_side_effects=True, vmem_limit_bytes=63 * 2**20
+            collective_id=0, has_side_effects=True, vmem_limit_bytes=52 * 2**20
         ),
     )(state, w_qkv, norm_gain, seg, w_out, probe, noise)
 

time: 131 us -> 128 us (0.977)
  Pallas kernels: 128 us -> 124 us
    pallas_call x1, Pallas kernels: 128 us -> 124 us  [heads_body(): pl.pallas_call(functools.partial(step_kernel, ctx_count, head_count), out...]
    unnamed x1 -> x7, local copies, waits for them, and re-layouts: 2.3 us -> 3.39 us
where the time goes in v4:
time: 128 us; the launch traced here: 127 us
  Pallas kernels  124 us (97%)
  local copies, waits for them, and re-layouts  3.39 us (3%)
    pallas_call x1, Pallas kernels, heads_body(): pl.pallas_call(functools.partial(step_kernel, ctx_count, head_count), out...  124 us
    unnamed x7, local copies, waits for them, and re-layouts  3.39 us

profile of v4, /device:TPU:0, one launch (start us, length us, event | category | flops | bytes accessed | tf_op | source)
XLA Modules:
  0.0 127.5 jit_solution(4430855462228623382)
XLA Ops:
  0.0 0.0 copy-start
  0.0 1.0 copy-done
  1.0 0.0 copy-start.1
  1.0 0.7 copy-done.1
  1.7 0.0 copy-start.2
  1.7 0.7 copy-done.2
  2.4 124.1 %shard_map.73 = f32[128,2048]{1,0:T(8,128)S(1)} custom-call(bf16[1024,2048]{1,0:T(8,128)(2,1)} %state_any.1, bf16[3,2048,256]{2,1,0:T(8,128)(2,1)} %w_any.1, bf16[2048]{0:T(1024)(128)(2,1)S(1)} %copy-done.1, s32[8,128]{1,0:T(8,128)S(1)} %bitcast.1, bf16[256,2048]{1,0:T(8,128)(2,1)} %w_out_any.1, bf16[1024,2048]{1,0:T(8,128)(2,1)} %probe_any.1, ...), custom_call_target="tpu_custom_call" | custom-call | tf_op jit(solution)/shard_map/pallas_call | solution.py:1516
  126.5 1.0 copy.9
Async XLA Ops:
  0.0 1.0 copy-start
  1.0 0.7 copy-start.1
  1.7 0.7 copy-start.2

commit v5 on v4

--- a/solution.py
+++ b/solution.py
@@ -1029,12 +1029,9 @@
             else:
                 out_copy(tile, order, other).start()
 
-        @pl.when(tile == 1)
-        def _():
-            line_arrived(2, 1)
-
-        return 0
-
+        return 0
+
+    line_arrived(2, 1)
     lax.fori_loop(0, ctx_count, one_tile, 0)
     for copy in later_loads:
         copy.wait()

time: 128 us -> 127 us (level)
  no operation moved by 1% of the time
where the time goes in v5:
time: 127 us
  Pallas kernels  124 us (98%)
  local copies, waits for them, and re-layouts  3.39 us (3%)
    pallas_call x1, Pallas kernels, heads_body(): pl.pallas_call(functools.partial(step_kernel, ctx_count, head_count), out...  124 us
    unnamed x7, local copies, waits for them, and re-layouts  3.39 us

profile of v5, /device:TPU:0, one launch (start us, length us, event | category | flops | bytes accessed | tf_op | source)
XLA Modules:
  0.0 127.0 jit_solution(9361486441429440452)
XLA Ops:
  0.0 0.0 copy-start
  0.0 1.0 copy-done
  1.0 0.0 copy-start.1
  1.0 0.7 copy-done.1
  1.7 0.0 copy-start.2
  1.7 0.7 copy-done.2
  2.4 123.6 %shard_map.73 = f32[128,2048]{1,0:T(8,128)S(1)} custom-call(bf16[1024,2048]{1,0:T(8,128)(2,1)} %state_any.1, bf16[3,2048,256]{2,1,0:T(8,128)(2,1)} %w_any.1, bf16[2048]{0:T(1024)(128)(2,1)S(1)} %copy-done.1, s32[8,128]{1,0:T(8,128)S(1)} %bitcast.1, bf16[256,2048]{1,0:T(8,128)(2,1)} %w_out_any.1, bf16[1024,2048]{1,0:T(8,128)(2,1)} %probe_any.1, ...), custom_call_target="tpu_custom_call" | custom-call | tf_op jit(solution)/shard_map/pallas_call | solution.py:1513
  126.0 1.0 copy.9
Async XLA Ops:
  0.0 1.0 copy-start
  1.0 0.7 copy-start.1
  1.7 0.7 copy-start.2
